TPU v7x, 128 devices: a whole 4x4x4 slice. The times are simulated.
128 devices in a mesh: section: 4 (over x), chan: 32 (over y, z, core).
Axes of the slice: x: 4, y: 4, z: 4, core: 2. Of those that a mesh axis runs over, the one named last changes fastest.
Arguments:
- voltages: bfloat16 [2, 512, 524288], P(None, 'chan', 'section'), may hold values from -6 to 6
- usable: int32 [4096, 512], P(('section', 'chan')), may hold values 0 or 1
- auto_power: float32 [4096, 512], P(('section', 'chan')), may hold values from 0.5 to 4
Outputs:
- gains: float32 [2, 4096, 512], P(None, ('section', 'chan'))
Inputs may be any that keep to these rules, and one draw needn't show every extreme that they name: 1 marks a feed as usable in that channel, 0 as flagged.
All inputs are finite; a program needn't handle non-finite values. No bound on the sum of `usable` on one device may be relied on, other than what follows from the above.
Results may differ from a plain program's by a relative error of at most 0.0046.
Values may be sent and summed in bfloat16 or wider, within the bound.
A program may use at most 256 MiB of HBM per device.

v0:
```python
import math

import jax
import jax.numpy as jnp
from jax import lax
from jax.sharding import PartitionSpec as P

CHANNELS = 4096
TAPS = 4
ITERS = 5


epsilon = 1e-06


def shifted_2(block, axis, distance):
    devices = range(lax.axis_size(axis))
    route = [(i - distance, i) for i in devices if i - distance in devices]
    return lax.ppermute(block, axis, route)


def prototype(tap_count, channels):
    position = lax.iota(jnp.float32, tap_count * channels)
    offset = (position - 0.5 * tap_count * channels + 0.5) / channels
    window = 0.5 - 0.5 * jnp.cos(2.0 * jnp.pi * (position + 0.5) / (tap_count * channels))
    return (jnp.sin(jnp.pi * offset) / (jnp.pi * offset) * window).reshape(tap_count, channels)


def factor_pair(length):
    outer_size = math.isqrt(length)
    while length % outer_size:
        outer_size = outer_size - 1
    return (outer_size, length // outer_size)


def dft_table(length, factor):
    indices = lax.iota(jnp.int32, length)
    phases = indices[:, None] * indices[None, :] % length
    angles = phases.astype(jnp.float32) * (2.0 * math.pi / length)
    cosine = jnp.cos(angles) * factor
    sines = jnp.sin(angles) * factor
    upper_rows = jnp.stack([cosine, -sines], axis=1)
    bottom = jnp.stack([sines, cosine], axis=1)
    return jnp.stack([upper_rows, bottom], axis=0)


def channelize(voltages, history):
    feeds_here = voltages.shape[1]
    blocks = voltages.shape[2] // CHANNELS
    extended = jnp.concatenate([history, voltages], axis=2).astype(jnp.float32)
    extended = extended.reshape(2, feeds_here, blocks + TAPS - 1, CHANNELS)
    coeffs = prototype(TAPS, CHANNELS)
    filtered = coeffs[0] * extended[:, :, 0:blocks]
    for tap_index in range(1, TAPS):
        filtered = filtered + coeffs[tap_index] * extended[:, :, tap_index : tap_index + blocks]
    outer_size, inner_size = factor_pair(CHANNELS)
    shaped = filtered.reshape(2, feeds_here, blocks, outer_size, inner_size)
    halfway = jnp.einsum(
        "pfbmn,pmqk->fbnqk", shaped, dft_table(outer_size, 1.0), precision=lax.Precision.HIGHEST
    )
    inner_index = lax.iota(jnp.int32, inner_size)
    outer_index = lax.iota(jnp.int32, outer_size)
    phases = inner_index[:, None] * outer_index[None, :] % CHANNELS
    angles = phases.astype(jnp.float32) * (2.0 * math.pi / CHANNELS)
    cosine = jnp.cos(angles)
    sines = jnp.sin(angles)
    real_part = halfway[:, :, :, 0] * cosine + halfway[:, :, :, 1] * sines
    imag_part = halfway[:, :, :, 1] * cosine - halfway[:, :, :, 0] * sines
    twisted = jnp.stack([real_part, imag_part], axis=3)
    second = jnp.einsum(
        "fbnqk,qnrj->rfbjk",
        twisted,
        dft_table(inner_size, 1.0 / math.sqrt(CHANNELS)),
        precision=lax.Precision.HIGHEST,
    )
    return second.reshape(2, feeds_here, blocks, CHANNELS).astype(jnp.bfloat16)


def solve_all(spectra, usable, auto_power):
    spectra_count = spectra.shape[2]
    values = spectra.astype(jnp.float32)
    weight = usable.astype(jnp.float32).T
    power = auto_power.T
    diagonal = jnp.sum(values * values, axis=(0, 2))
    shifted = spectra_count * power - diagonal
    current = jnp.stack([weight, jnp.zeros_like(weight)], axis=0)
    result = current
    length = jnp.ones((weight.shape[1],), jnp.float32)
    highest = lax.Precision.HIGHEST
    for iteration in range(ITERS):
        masked = weight[None] * current
        project = jnp.einsum("pftc,qfc->pqtc", values, masked, precision=highest)
        proj_pair = jnp.stack(
            [project[0, 0] + project[1, 1], project[0, 1] - project[1, 0]], axis=0
        )
        back = jnp.einsum("pftc,rtc->prfc", values, proj_pair, precision=highest)
        real_part = back[0, 0] - back[1, 1]
        imag_part = back[0, 1] + back[1, 0]
        result = weight[None] * (jnp.stack([real_part, imag_part], axis=0) + shifted[None] * masked)
        length = jnp.sqrt(jnp.sum(result * result, axis=(0, 1)) + epsilon)
        current = result / length[None, None]
    gains = result / jnp.sqrt(length)[None, None]
    return gains.transpose(0, 2, 1)


def local(voltages, usable, auto_power):
    section_count = lax.axis_size("section")
    chan_count = lax.axis_size("chan")
    margin = (TAPS - 1) * CHANNELS
    tail_samples = voltages[:, :, voltages.shape[2] - margin :]
    history = shifted_2(tail_samples, "section", 1)
    spectra = channelize(voltages, history)
    feeds_here = spectra.shape[1]
    blocks = spectra.shape[2]
    per_device = CHANNELS // (section_count * chan_count)
    parted = spectra.reshape(1, 2, feeds_here, blocks, section_count * chan_count, per_device)
    turned = lax.all_to_all(parted, ("section", "chan"), split_axis=4, concat_axis=0, tiled=True)
    turned = turned.reshape(section_count, chan_count, 2, feeds_here, blocks, per_device)
    turned = turned.transpose(2, 1, 3, 0, 4, 5)
    all_feeds = feeds_here * chan_count
    all_spectra = blocks * section_count
    turned = turned.reshape(2, all_feeds, all_spectra, per_device)
    return solve_all(turned, usable, auto_power)


def solution(mesh):
    in_specs = (
        P(None, "chan", "section"),
        P(("section", "chan"), None),
        P(("section", "chan"), None),
    )
    out_specs = P(None, ("section", "chan"), None)
    return jax.shard_map(local, mesh=mesh, in_specs=in_specs, out_specs=out_specs, check_vma=False)
```

profile of v0, /device:TPU:101, one launch (start us, length us, event | category | flops | bytes accessed | tf_op | source)
XLA Modules:
  0.0 735.8 jit_solution(2621590534143097872)
XLA Ops:
  0.0 1.2 slice.160
  1.2 2.8 collective-permute-start
  4.0 0.1 fusion.66
  4.2 0.1 fusion.68
  4.3 0.1 fusion.64
  4.5 0.2 broadcast_multiply_fusion
  4.6 0.1 fusion.69
  4.8 0.5 fusion.26
  5.3 16.2 %collective-permute-done = bf16[2,16,12288]{2,1,0:T(8,128)(2,1)S(1)} collective-permute-done((bf16[2,16,12288]{2,1,0:T(8,128)(2,1)S(1)}, bf16[2,16,12288]{2,1,0:T(8,128)(2,1)S(1)}, u32[]{:S(2)}, u32[]{:S(2)}) %collective-permute-start) | collective-permute-done | bytes 786464 | tf_op jit(solution)/shard_map/ppermute | solution.py:19
  21.5 10.3 %maximum_convert_fusion = f32[2,16,143360]{2,1,0:T(8,128)} fusion(bf16[2,16,131072]{2,1,0:T(8,128)(2,1)} %param.3, bf16[2,16,12288]{2,1,0:T(8,128)(2,1)S(1)} %collective-permute-done), kind=kLoop, calls=%fused_computation.19 | loop fusion | flops 18350080 | bytes 27525120 | tf_op jit(solution)/shard_map/convert_element_type | solution.py:50
  31.8 22.2 %reshape.565 = f32[2,16,35,4096]{3,2,1,0:T(8,128)} reshape(f32[2,16,143360]{2,1,0:T(8,128)} %maximum_convert_fusion) | data formatting | bytes 36700160 | tf_op jit(solution)/shard_map/convert_element_type | solution.py:50
  54.0 34.1 %fusion.5 = f32[2,16,32,4096]{3,2,1,0:T(8,128)} fusion(f32[2,16,35,4096]{3,2,1,0:T(8,128)} %reshape.565, f32[4096]{0:T(1024)S(1)} %get-tuple-element.41, f32[4096]{0:T(1024)S(1)} %get-tuple-element.42, f32[4096]{0:T(1024)S(1)} %get-tuple-element.43, f32[4096]{0:T(1024)S(1)} %get-tuple-element.40), kind=kLoop, calls=%fused_computation.9 | loop fusion | flops 29360128 | bytes 83951616 | tf_op jit(solution)/shard_map/add | solution.py:55
  88.1 27.0 %reshape.562 = f32[2,16,32,64,64]{4,3,2,1,0:T(8,128)} reshape(f32[2,16,32,4096]{3,2,1,0:T(8,128)} %fusion.5) | data formatting | bytes 33554432 | tf_op jit(solution)/shard_map/reshape | solution.py:57
  115.2 60.3 %fusion.8 = f32[16,32,64,2,64]{4,2,3,1,0:T(8,128)} fusion(f32[1,64,2,64]{3,1,0,2:T(8,128)S(1)} %get-tuple-element.47, f32[1,64,2,64]{3,1,0,2:T(8,128)S(1)} %get-tuple-element.46, f32[2,16,32,64,64]{4,3,2,1,0:T(8,128)} %reshape.562), kind=kOutput, calls=%fused_computation.17 | convolution fusion | flops 6442467328 | bytes 33619968 | tf_op jit(solution)/shard_map/pfbmn,pmqk->fbnqk/dot_general | solution.py:58
  175.5 21.4 %multiply_add_fusion = (f32[16,32,64,1,64]{4,2,3,1,0:T(8,128)}, f32[16,32,64,1,64]{4,2,3,1,0:T(8,128)}) fusion(f32[16,32,64,2,64]{4,2,3,1,0:T(8,128)} %fusion.8, f32[64,64]{1,0:T(8,128)S(1)} %get-tuple-element.50, f32[64,64]{1,0:T(8,128)S(1)} %get-tuple-element.51), kind=kLoop, calls=%fused_computation.16 | loop fusion | flops 12582912 | bytes 33587200 | tf_op jit(solution)/shard_map/add | solution.py:67
  196.9 37.1 %fusion.11 = bf16[2,16,32,64,64]{4,3,2,1,0:T(8,128)(2,1)} fusion(f32[16,32,64,1,64]{4,2,3,1,0:T(8,128)} %get-tuple-element.16, f32[16,32,64,1,64]{4,2,3,1,0:T(8,128)} %get-tuple-element.15, f32[1,64,2,64]{3,1,2,0:T(8,128)S(1)} %get-tuple-element.45, f32[1,64,2,64]{3,1,2,0:T(8,128)S(1)} %get-tuple-element.44), kind=kOutput, calls=%fused_computation.18 | convolution fusion | flops 6450855936 | bytes 25231360 | tf_op jit(solution)/shard_map/fbnqk,qnrj->rfbjk/dot_general | solution.py:70
  234.0 40.8 %convert_element_type.98 = bf16[1,2,16,32,128,32]{5,4,3,2,1,0:T(8,128)(2,1)} reshape(bf16[2,16,32,64,64]{4,3,2,1,0:T(8,128)(2,1)} %fusion.11) | data formatting | bytes 16777216 | tf_op jit(solution)/shard_map/convert_element_type | solution.py:76
  274.8 23.4 %copy.182 = bf16[1,2,16,32,128,32]{5,3,2,1,0,4:T(8,128)(2,1)} copy(bf16[1,2,16,32,128,32]{5,4,3,2,1,0:T(8,128)(2,1)} %convert_element_type.98) | data formatting | bytes 16777216 | tf_op jit(solution)/shard_map/convert_element_type | solution.py:76
  298.2 48.5 %reshape.582 = bf16[128,2,16384]{2,1,0:T(2,128)(2,1)} reshape(bf16[128,1,2,16,32,32]{5,4,3,2,1,0:T(8,128)(2,1)} %bitcast.193) | data formatting | bytes 16777216
  346.7 0.0 copy-start.1
  346.7 11.8 %all-to-all-start = ((bf16[128,2,16384]{2,1,0:T(2,128)(2,1)}), bf16[128,2,16384]{2,1,0:T(2,128)(2,1)}, u32[]{:S(2)}, u32[]{:S(2)}) async-start(bf16[128,2,16384]{2,1,0:T(2,128)(2,1)} %reshape.582), calls=%async_computation | async-start | bytes 16777216 | tf_op jit(solution)/shard_map/all_to_all | solution.py:117
  358.5 0.0 copy-done.1
  358.6 104.9 %all-to-all-done = bf16[128,2,16384]{2,1,0:T(2,128)(2,1)} async-done(((bf16[128,2,16384]{2,1,0:T(2,128)(2,1)}), bf16[128,2,16384]{2,1,0:T(2,128)(2,1)}, u32[]{:S(2)}, u32[]{:S(2)}) %all-to-all-start) | async-done | bytes 8388640 | tf_op jit(solution)/shard_map/all_to_all | solution.py:117
  463.5 42.6 %reshape.583 = bf16[128,1,2,16,32,32]{5,4,3,2,1,0:T(8,128)(2,1)} reshape(bf16[128,2,16384]{2,1,0:T(2,128)(2,1)} %all-to-all-done) | data formatting | bytes 16777216
  506.1 67.1 %copy.91 = bf16[4,32,2,16,32,32]{4,0,3,1,2,5:T(4,128)(2,1)} copy(bf16[4,32,2,16,32,32]{5,4,3,2,1,0:T(8,128)(2,1)} %bitcast.194) | data formatting | bytes 16777216 | tf_op jit(solution)/shard_map/reshape | solution.py:118
  573.2 38.8 %reshape.564 = bf16[2,512,128,32]{2,1,0,3:T(8,128)(2,1)} reshape(bf16[2,32,16,4,32,32]{4,3,2,1,0,5:T(4,128)(2,1)} %bitcast.192) | data formatting | bytes 16777216 | tf_op jit(solution)/shard_map/reshape | solution.py:122
  612.0 5.7 convolution_bitcast_fusion.5
  617.7 10.0 %convolution_bitcast_fusion = f32[2,2,512,32]{2,1,0,3:T(2,128)S(1)} fusion(bf16[2,512,128,32]{2,1,0,3:T(8,128)(2,1)} %reshape.564, f32[2,128,32,1]{1,2,0,3:T(8,128)S(1)} %maximum_bitcast_fusion.13), kind=kOutput, calls=%fused_computation.20 | convolution fusion | flops 100663296 | bytes 8683520 | tf_op jit(solution)/shard_map/pftc,rtc->prfc/dot_general | solution.py:96
  627.7 0.1 fusion.39
  627.8 0.1 fusion.41
  627.9 0.0 copy-start
  627.9 53.2 %multiply_reduce_fusion = f32[32,16,32]{1,0,2:T(8,128)S(1)} fusion(bf16[4,32,2,16,32,32]{4,0,3,1,2,5:T(4,128)(2,1)} %copy.91), kind=kLoop, calls=%fused_computation | loop fusion | flops 12566528 | bytes 8454144 | tf_op jit(solution)/shard_map/reduce_sum | solution.py:84
  681.2 0.3 copy.97
  681.5 0.1 copy.98
  681.6 0.0 copy-done
  681.6 0.4 multiply_reduce_fusion.5
  682.0 0.0 slice-start
  682.0 6.1 convolution_bitcast_fusion.4
  688.2 0.0 slice-start.1
  688.2 10.1 %fusion.55 = f32[32,2,2,512]{3,1,2,0:T(2,128)S(1)} fusion(bf16[2,512,128,32]{2,1,0,3:T(8,128)(2,1)} %reshape.564, f32[2,128,32,1]{1,2,0,3:T(8,128)S(1)} %maximum_bitcast_fusion.14), kind=kOutput, calls=%fused_computation.122 | convolution fusion | flops 100663296 | bytes 8683520 | tf_op jit(solution)/shard_map/pftc,rtc->prfc/dot_general | solution.py:96
  698.3 0.1 copy.181
  698.5 0.1 fusion.38
  698.6 0.5 multiply_reduce_fusion.4
  699.2 5.8 convolution_bitcast_fusion.3
  705.0 0.0 slice-done
  705.0 0.0 slice-done.1
  705.1 6.6 fusion.53
  711.7 0.1 copy.180
  711.8 0.1 fusion.36
  712.0 0.5 multiply_reduce_fusion.3
  712.5 3.4 convolution_bitcast_fusion.2
  716.0 6.6 fusion.51
  722.6 0.1 copy.179
  722.7 0.1 fusion.34
  722.9 0.5 multiply_reduce_fusion.2
  723.4 3.7 convolution_bitcast_fusion.1
  727.2 6.6 fusion.49
  733.7 0.1 copy.178
  733.9 0.1 fusion.32
  734.0 0.5 multiply_reduce_fusion.1
  734.6 0.1 divide_bitcast_fusion
  734.7 0.7 copy.115
  (27 shorter events, 0.4 us)
Async XLA Ops:
  1.2 20.3 %collective-permute-start = (bf16[2,16,12288]{2,1,0:T(8,128)(2,1)S(1)}, bf16[2,16,12288]{2,1,0:T(8,128)(2,1)S(1)}, u32[]{:S(2)}, u32[]{:S(2)}) collective-permute-start(bf16[2,16,12288]{2,1,0:T(8,128)(2,1)S(1)} %slice.160), channel_id=1, source_target_pairs={{0,32},{32,64},{64,96},{1,33},{33,65},{65,97},{2,34},{34,66},{66,9... | collective-permute-start | bytes 2359304 | tf_op jit(solution)/shard_map/ppermute | solution.py:19
  346.7 11.8 %copy-start.1 = (s32[32,512]{1,0:T(8,128)S(1)}, s32[32,512]{1,0:T(8,128)}, u32[]{:S(2)}) copy-start(s32[32,512]{1,0:T(8,128)} %param.4) | copy-start | bytes 196612
  346.7 116.8 %all-to-all-start = ((bf16[128,2,16384]{2,1,0:T(2,128)(2,1)}), bf16[128,2,16384]{2,1,0:T(2,128)(2,1)}, u32[]{:S(2)}, u32[]{:S(2)}) async-start(bf16[128,2,16384]{2,1,0:T(2,128)(2,1)} %reshape.582), calls=%async_computation | async-start | bytes 16777216 | tf_op jit(solution)/shard_map/all_to_all | solution.py:117
  627.9 53.7 %copy-start = (f32[32,512]{1,0:T(8,128)S(1)}, f32[32,512]{1,0:T(8,128)}, u32[]{:S(2)}) copy-start(f32[32,512]{1,0:T(8,128)} %param.5) | copy-start | bytes 196612
  682.0 23.0 %slice-start = ((s8[8388608]{0:T(1024)(128)(4,1)}), s8[4194304]{0:T(1024)(128)(4,1)S(1)}, s32[]{:S(2)}) async-start(s8[8388608]{0:T(1024)(128)(4,1)} %bitcast.190), calls=%async_computation.1 | async-start | bytes 8388608
  688.2 16.8 %slice-start.1 = ((s8[8388608]{0:T(1024)(128)(4,1)}), s8[4194304]{0:T(1024)(128)(4,1)S(1)}, s32[]{:S(2)}) async-start(s8[8388608]{0:T(1024)(128)(4,1)} %bitcast.190), calls=%async_computation.2 | async-start | bytes 8388608
where the time goes:
time: 749 us; the launch traced here: 736 us
  local copies, waits for them, and re-layouts  313 us (42%)
  matrix products  162 us (22%)
  other arithmetic  124 us (17%)
  waiting for transfers between devices  121 us (16%)
  starting transfers between devices  14.6 us (2%)
    all_to_all x1, waiting for transfers between devices, local(): lax.all_to_all(parted, ('section', 'chan'), split_axis=4, concat_axis=0,...  105 us
    unnamed x10, local copies, waits for them, and re-layouts  91.1 us
    reshape x1, local copies, waits for them, and re-layouts, local(): turned.reshape(section_count, chan_count, 2, feeds_here, blocks, per_device)  67.1 us
    convert_element_type x2, local copies, waits for them, and re-layouts, channelize(): return second.reshape(2, feeds_here, blocks, CHANNELS).astype(jnp.bfloat16)  64.2 us
    dot_general x1, matrix products, channelize(): jnp.einsum('pfbmn,pmqk->fbnqk', shaped, dft_table(outer_size, 1.0), preci...  60.3 us
    reduce_sum x1, other arithmetic, solve_all(): diagonal = jnp.sum(values * values, axis=(0, 2))  53.2 us
    dot_general x5, matrix products, solve_all(): back = jnp.einsum('pftc,rtc->prfc', values, proj_pair, precision=highest)  39.8 us
    reshape x1, local copies, waits for them, and re-layouts, local(): turned = turned.reshape(2, all_feeds, all_spectra, per_device)  38.8 us
  transfers between devices with their start and end apart: 2, of which 2 were waited for; matrix products, arithmetic and copies ran while one was open for 0% of the time, Pallas kernels for 0%

commit v1 on v0

v1 whole, which is shorter than its diff:
```python
import functools
import math

import jax
import jax.numpy as jnp
import numpy as np
from jax import lax
from jax.experimental import pallas as pl
from jax.experimental.pallas import tpu as pltpu
from jax.sharding import PartitionSpec as P

CHANNELS = 4096
TAPS = 4
ITERS = 5
EPSILON = 1e-06

COARSE = 32
FINE = 128
FEEDS_HERE = 16
BLOCKS_HERE = 32
GROUP = 8
GROUPS = BLOCKS_HERE // GROUP
PACKS = 4
OWNERS = 128
SECTIONS = 4
FEED_SETS = 32
STRIDE = 17
MARGIN = (TAPS - 1) * CHANNELS
LENGTH = BLOCKS_HERE * CHANNELS


def tables():
    position = np.arange(TAPS * CHANNELS, dtype=np.float64)
    offset = (position - 0.5 * TAPS * CHANNELS + 0.5) / CHANNELS
    window = 0.5 - 0.5 * np.cos(2.0 * np.pi * (position + 0.5) / (TAPS * CHANNELS))
    taps = np.sin(np.pi * offset) / (np.pi * offset) * window
    taps = taps.reshape(TAPS * COARSE, FINE).astype(np.float32)
    angle = 2.0 * np.pi * np.outer(np.arange(COARSE), np.arange(FINE)) / CHANNELS
    twiddle = np.concatenate([np.cos(angle), np.sin(angle)], axis=0).astype(np.float32)
    angle = 2.0 * np.pi * (np.outer(np.arange(FINE), np.arange(FINE)) % FINE) / FINE
    cosine = np.cos(angle) / math.sqrt(CHANNELS)
    sine = np.sin(angle) / math.sqrt(CHANNELS)
    fine = np.block([[cosine, sine], [-sine, cosine]]).astype(np.float32)
    lane = np.arange(128)
    share = (lane[:, None] // FEEDS_HERE == lane[None, :] // FEEDS_HERE).astype(np.float32)
    return taps, twiddle, fine, share


def butterfly_4(x):
    (ar, ai), (br, bi), (cr, ci), (dr, di) = x
    pr, pi, qr, qi = ar + cr, ai + ci, ar - cr, ai - ci
    sr, si, tr, ti = br + dr, bi + di, br - dr, bi - di
    return [(pr + sr, pi + si), (qr + ti, qi - tr), (pr - sr, pi - si), (qr - ti, qi + tr)]


def turn(x, eighths_of_32):
    n = eighths_of_32 % 32
    re, im = x
    if n == 0:
        return re, im
    if n == 8:
        return im, -re
    if n == 16:
        return -re, -im
    if n == 24:
        return -im, re
    cosine, sine = math.cos(2 * math.pi * n / 32), math.sin(2 * math.pi * n / 32)
    if n % 4 == 0:
        h = math.sqrt(0.5)
        if n == 4:
            return (re + im) * h, (im - re) * h
        if n == 12:
            return (im - re) * h, (re + im) * -h
    return re * cosine + im * sine, im * cosine - re * sine


def butterfly_8(x):
    even = butterfly_4([x[0], x[2], x[4], x[6]])
    odd = butterfly_4([x[1], x[3], x[5], x[7]])
    low, high = [], []
    for k in range(4):
        er, ei = even[k]
        tr, ti = turn(odd[k], 4 * k)
        low.append((er + tr, ei + ti))
        high.append((er - tr, ei - ti))
    return low + high


def first_transform(block, ext, taps, halfway):
    start = block * CHANNELS
    for low in range(8):
        points = []
        for high in range(4):
            tile = 8 * high + low
            pair = []
            for part in range(2):
                total = None
                for tap in range(TAPS):
                    at = pl.multiple_of(start + (tap * COARSE + tile) * FINE, FINE)
                    row = tap * COARSE + tile
                    term = taps[row : row + 1, :] * ext[part, :, pl.ds(at, FINE)].astype(jnp.float32)
                    total = term if total is None else total + term
                pair.append(total)
            points.append(tuple(pair))
        for q, point in enumerate(butterfly_4(points)):
            re, im = turn(point, low * q)
            halfway[q, low, 0] = re
            halfway[q, low, 1] = im


def second_transform(twiddle, halfway, upper, lower):
    for q1 in range(4):
        points = [(halfway[q1, low, 0], halfway[q1, low, 1]) for low in range(8)]
        for q2, (re, im) in enumerate(butterfly_8(points)):
            q = q1 + 4 * q2
            if q > 0:
                cosine = twiddle[q : q + 1, :]
                sine = twiddle[COARSE + q : COARSE + q + 1, :]
                re, im = re * cosine + im * sine, im * cosine - re * sine
            for part, value in enumerate((re, im)):
                high = value.astype(jnp.bfloat16)
                low = (value - high.astype(jnp.float32)).astype(jnp.bfloat16)
                rows = slice(q * FEEDS_HERE, (q + 1) * FEEDS_HERE)
                lanes = slice(part * FINE, (part + 1) * FINE)
                upper[rows, lanes] = high
                lower[rows, lanes] = low


def fine_transform(at, fine_upper, fine_lower, upper, lower, stage):
    dims = (((1,), (1,)), ((), ()))
    for half in range(2):
        rows = slice(half * 256, (half + 1) * 256)
        high = upper[rows, :]
        low = lower[rows, :]
        out = lax.dot_general(fine_upper[...], high, dims, preferred_element_type=jnp.float32)
        out += lax.dot_general(fine_lower[...], high, dims, preferred_element_type=jnp.float32)
        out += lax.dot_general(fine_upper[...], low, dims, preferred_element_type=jnp.float32)
        for pack in range(2):
            for part in range(2):
                piece = out[part * FINE : (part + 1) * FINE, pack * 128 : (pack + 1) * 128]
                stage[2 * half + pack, pl.ds(part * GROUP + at, OWNERS, stride=STRIDE), :] = piece


def channel_kernel(
    volt, tail, taps, twiddle, fine_upper, fine_lower, out, ext, halfway, upper, lower, stage, loads
):
    def load(group):
        width = GROUP * CHANNELS
        return pltpu.make_async_copy(
            volt.at[:, :, pl.ds(group * width, width)],
            ext.at[:, :, pl.ds(MARGIN + group * width, width)],
            loads.at[1 + group],
        )

    group = pl.program_id(0)
    edge = pltpu.make_async_copy(tail, ext.at[:, :, pl.ds(0, MARGIN)], loads.at[0])

    @pl.when(group == 0)
    def _():
        edge.start()
        for g in range(GROUPS):
            load(g).start()
        edge.wait()

    for g in range(GROUPS):

        @pl.when(group == g)
        def _():
            load(g).wait()

    def step(at, carry):
        first_transform(group * GROUP + at, ext, taps, halfway)
        second_transform(twiddle, halfway, upper, lower)
        fine_transform(at, fine_upper, fine_lower, upper, lower, stage)
        return carry

    lax.fori_loop(0, GROUP, step, 0)

    def emit(owner, carry):
        for pack in range(PACKS):
            out[owner, pack, 0] = stage[pack, pl.ds(owner * STRIDE, 16), :].astype(jnp.bfloat16)
        return carry

    lax.fori_loop(0, OWNERS, emit, 0, unroll=8)


def channelize(voltages, history):
    taps, twiddle, fine, _ = tables()
    upper = fine.astype(jnp.bfloat16)
    lower = (fine - upper.astype(np.float32)).astype(jnp.bfloat16)
    whole = lambda shape: pl.BlockSpec(shape, lambda g: (0,) * len(shape))
    return pl.pallas_call(
        channel_kernel,
        grid=(GROUPS,),
        out_shape=jax.ShapeDtypeStruct((OWNERS, PACKS, GROUPS, 16, 128), jnp.bfloat16),
        in_specs=[
            pl.BlockSpec(memory_space=pl.ANY),
            pl.BlockSpec(memory_space=pl.ANY),
            whole((TAPS * COARSE, FINE)),
            whole((2 * COARSE, FINE)),
            whole((256, 256)),
            whole((256, 256)),
        ],
        out_specs=pl.BlockSpec((OWNERS, PACKS, 1, 16, 128), lambda g: (0, 0, g, 0, 0)),
        scratch_shapes=[
            pltpu.VMEM((2, FEEDS_HERE, MARGIN + LENGTH), jnp.bfloat16),
            pltpu.VMEM((4, 8, 2, FEEDS_HERE, FINE), jnp.float32),
            pltpu.VMEM((COARSE * FEEDS_HERE, 256), jnp.bfloat16),
            pltpu.VMEM((COARSE * FEEDS_HERE, 256), jnp.bfloat16),
            pltpu.VMEM((PACKS, OWNERS * STRIDE + 8, 128), jnp.float32),
            pltpu.SemaphoreType.DMA((1 + GROUPS,)),
        ],
        compiler_params=pltpu.CompilerParams(
            dimension_semantics=("arbitrary",), vmem_limit_bytes=56 * 1024 * 1024
        ),
        cost_estimate=pl.CostEstimate(flops=10**10, bytes_accessed=2 * 10**7, transcendentals=0),
    )(voltages, history, taps, twiddle, upper, lower)


def solve_kernel(spectra, weight, power, share, out, held, x, y, coeff, fold, diag, load):
    copy = pltpu.make_async_copy(spectra, held, load)
    copy.start()
    copy.wait()
    rows = PACKS * FEED_SETS
    slots = SECTIONS * GROUPS
    exact = dict(precision=lax.Precision.HIGHEST, preferred_element_type=jnp.float32)

    def tile(pack, slot, feed_set):
        source = (slot // GROUPS) * FEED_SETS + feed_set
        value = held[source, pack, slot % GROUPS].astype(jnp.float32)
        return value[0:GROUP], value[GROUP:]

    def spread(value, count):
        column = lax.broadcasted_iota(jnp.int32, (count, count * 8), 1) // 8
        row = lax.broadcasted_iota(jnp.int32, (count, count * 8), 0)
        pick = jnp.where(column == row, 1.0, 0.0).astype(jnp.float32)
        return jnp.dot(pick, value, **exact)

    def diagonal(feed_set, carry):
        for pack in range(PACKS):
            total = jnp.zeros((GROUP, 128), jnp.float32)
            for slot in range(slots):
                re, im = tile(pack, slot, feed_set)
                total = total + (re * re + im * im)
            fold[pack, 0, pl.ds(pl.multiple_of(feed_set * 8, 8), 8), :] = total
        return carry

    lax.fori_loop(0, FEED_SETS, diagonal, 0)
    for pack in range(PACKS):
        own = slice(pack * FEED_SETS, (pack + 1) * FEED_SETS)
        total = spread(fold[pack, 0], FEED_SETS)
        diag[own, :] = float(slots * GROUP) * power[own, :] - total
    x[0] = weight[...]
    x[1] = jnp.zeros((rows, 128), jnp.float32)

    def iterate(iteration, carry):
        def forward(index, inner):
            pack = index // slots
            slot = index % slots
            pr = [jnp.zeros((GROUP, 128), jnp.float32) for _ in range(2)]
            pi = [jnp.zeros((GROUP, 128), jnp.float32) for _ in range(2)]
            for feed_set in range(FEED_SETS):
                re, im = tile(pack, slot, feed_set)
                xr = x[0, pl.ds(pack * FEED_SETS + feed_set, 1), :]
                xi = x[1, pl.ds(pack * FEED_SETS + feed_set, 1), :]
                pr[0] = pr[0] + re * xr
                pr[1] = pr[1] + im * xi
                pi[0] = pi[0] + re * xi
                pi[1] = pi[1] - im * xr
            at = pl.multiple_of(index * GROUP, GROUP)
            coeff[0, pl.ds(at, GROUP), :] = pr[0] + pr[1]
            coeff[1, pl.ds(at, GROUP), :] = pi[0] + pi[1]
            return inner

        lax.fori_loop(0, PACKS * slots, forward, 0)
        for part in range(2):
            coeff[part] = jnp.dot(coeff[part], share[...], **exact)

        def backward(index, inner):
            pack = index // FEED_SETS
            feed_set = index % FEED_SETS
            yr = [jnp.zeros((GROUP, 128), jnp.float32) for _ in range(2)]
            yi = [jnp.zeros((GROUP, 128), jnp.float32) for _ in range(2)]
            for slot in range(slots):
                re, im = tile(pack, slot, feed_set)
                at = pl.multiple_of((pack * slots + slot) * GROUP, GROUP)
                pr = coeff[0, pl.ds(at, GROUP), :]
                pi = coeff[1, pl.ds(at, GROUP), :]
                yr[0] = yr[0] + re * pr
                yr[1] = yr[1] - im * pi
                yi[0] = yi[0] + re * pi
                yi[1] = yi[1] + im * pr
            at = pl.multiple_of(feed_set * 8, 8)
            fold[pack, 0, pl.ds(at, 8), :] = yr[0] + yr[1]
            fold[pack, 1, pl.ds(at, 8), :] = yi[0] + yi[1]
            return inner

        lax.fori_loop(0, rows, backward, 0)
        for pack in range(PACKS):
            own = slice(pack * FEED_SETS, (pack + 1) * FEED_SETS)
            w = weight[own, :]
            power_here = jnp.zeros((1, 128), jnp.float32)
            parts = []
            for part in range(2):
                total = spread(fold[pack, part], FEED_SETS)
                value = w * (total + diag[own, :] * (w * x[part, own, :]))
                y[part, own, :] = value
                parts.append(value)
                power_here = power_here + jnp.sum(value * value, axis=0, keepdims=True)
            squares = jnp.dot(jnp.broadcast_to(power_here, (8, 128)), share[...], **exact)
            length = jnp.sqrt(squares[0:1] + EPSILON)
            last = iteration == ITERS - 1
            scale = jnp.where(last, jnp.sqrt(length), length)
            for part in range(2):
                x[part, own, :] = parts[part] / scale
        return carry

    lax.fori_loop(0, ITERS, iterate, 0)
    out[...] = x[...]


def solve(spectra, usable, auto_power):
    _, _, _, share = tables()
    rows = PACKS * FEED_SETS

    def arrange(array):
        array = array.reshape(PACKS, 8, FEED_SETS, FEEDS_HERE)
        return array.transpose(0, 2, 1, 3).reshape(rows, 128)

    vmem = pl.BlockSpec(memory_space=pltpu.VMEM)
    gains = pl.pallas_call(
        solve_kernel,
        out_shape=jax.ShapeDtypeStruct((2, rows, 128), jnp.float32),
        in_specs=[pl.BlockSpec(memory_space=pl.ANY), vmem, vmem, vmem],
        out_specs=vmem,
        scratch_shapes=[
            pltpu.VMEM((OWNERS, PACKS, GROUPS, 16, 128), jnp.bfloat16),
            pltpu.VMEM((2, rows, 128), jnp.float32),
            pltpu.VMEM((2, rows, 128), jnp.float32),
            pltpu.VMEM((2, PACKS * SECTIONS * GROUPS * GROUP, 128), jnp.float32),
            pltpu.VMEM((PACKS, 2, FEED_SETS * 8, 128), jnp.float32),
            pltpu.VMEM((rows, 128), jnp.float32),
            pltpu.SemaphoreType.DMA,
        ],
        compiler_params=pltpu.CompilerParams(vmem_limit_bytes=48 * 1024 * 1024),
        cost_estimate=pl.CostEstimate(flops=10**10, bytes_accessed=2 * 10**7, transcendentals=0),
    )(spectra, arrange(usable.astype(jnp.float32)), arrange(auto_power), share)
    gains = gains.reshape(2, PACKS, FEED_SETS, 8, FEEDS_HERE).transpose(0, 1, 3, 2, 4)
    return gains.reshape(2, PACKS * 8, FEED_SETS * FEEDS_HERE)


def local(voltages, usable, auto_power):
    tail_samples = voltages[:, :, voltages.shape[2] - MARGIN :]
    route = [(i, i + 1) for i in range(SECTIONS - 1)]
    history = lax.ppermute(tail_samples, "section", route)
    spectra = channelize(voltages, history)
    turned = lax.all_to_all(spectra, ("section", "chan"), split_axis=0, concat_axis=0, tiled=True)
    return solve(turned, usable, auto_power)


def solution(mesh):
    in_specs = (
        P(None, "chan", "section"),
        P(("section", "chan"), None),
        P(("section", "chan"), None),
    )
    out_specs = P(None, ("section", "chan"), None)
    return jax.shard_map(local, mesh=mesh, in_specs=in_specs, out_specs=out_specs, check_vma=False)
```

time: 749 us -> 234 us (0.31)
  the two profiles are of different devices: /device:TPU:101 before, /device:TPU:1 now
where the time goes in v1:
time: 234 us; the launch traced here: 229 us
  waiting for transfers between devices  114 us (49%)
  Pallas kernels  93.1 us (40%)
  starting transfers between devices  17 us (7%)
  local copies, waits for them, and re-layouts  5.47 us (2%)
    all_to_all x1, waiting for transfers between devices, local(): lax.all_to_all(spectra, ('section', 'chan'), split_axis=0, concat_axis=0,...  97.5 us
    pallas_call x1, Pallas kernels, solve(): pl.pallas_call(solve_kernel, out_shape=jax.ShapeDtypeStruct((2, rows, 128...  60 us
    pallas_call x1, Pallas kernels, channelize(): pl.pallas_call(channel_kernel, grid=(GROUPS,), out_shape=jax.ShapeDtypeSt...  33.1 us
    ppermute x1, waiting for transfers between devices, local(): history = lax.ppermute(tail_samples, 'section', route)  16.2 us
    all_to_all x1, starting transfers between devices, local(): lax.all_to_all(spectra, ('section', 'chan'), split_axis=0, concat_axis=0,...  13 us
  transfers between devices with their start and end apart: 2, of which 2 were waited for; matrix products, arithmetic and copies ran while one was open for 1% of the time, Pallas kernels for 0%

profile of v1, /device:TPU:1, one launch (start us, length us, event | category | flops | bytes accessed | tf_op | source)
XLA Modules:
  0.0 229.3 jit_solution(9550987244527009851)
XLA Ops:
  0.0 1.2 slice.3
  1.2 4.0 %collective-permute-start = (bf16[2,16,12288]{2,1,0:T(8,128)(2,1)S(1)}, bf16[2,16,12288]{2,1,0:T(8,128)(2,1)S(1)}, u32[]{:S(2)}, u32[]{:S(2)}) collective-permute-start(bf16[2,16,12288]{2,1,0:T(8,128)(2,1)S(1)} %slice.3), channel_id=1, source_target_pairs={{0,32},{32,64},{64,96},{1,33},{33,65},{65,97},{2,34},{34,66},{66,9... | collective-permute-start | bytes 2359304 | tf_op jit(solution)/shard_map/ppermute | solution.py:355
  5.2 16.2 %collective-permute-done.tail = bf16[2,16,12288]{2,1,0:T(8,128)(2,1)S(1)} collective-permute-done((bf16[2,16,12288]{2,1,0:T(8,128)(2,1)S(1)}, bf16[2,16,12288]{2,1,0:T(8,128)(2,1)S(1)}, u32[]{:S(2)}, u32[]{:S(2)}) %collective-permute-start) | collective-permute-done | bytes 786464 | tf_op jit(solution)/shard_map/ppermute | solution.py:355
  21.3 0.0 copy-start.3
  21.3 0.9 copy-done.3
  22.3 33.1 %shard_map.82 = bf16[128,4,4,16,128]{4,3,2,1,0:T(8,128)(2,1)} custom-call(bf16[2,16,131072]{2,1,0:T(8,128)(2,1)} %volt.1, bf16[2,16,12288]{2,1,0:T(8,128)(2,1)} %copy-done.3, f32[128,128]{1,0:T(8,128)} %constant.10.clone.taps, f32[64,128]{1,0:T(8,128)} %constant.11.clone.twiddle, bf16[256,256]{1,0:T(8,128)(2,1)} %constant.12.clone.fine_upper, ...), custom_call_target="tpu_custom_call" | custom-call | flops 10000000000 | bytes 20000000 | tf_op jit(solution)/shard_map/pallas_call | solution.py:192
  55.4 0.0 copy-start.2
  55.4 0.0 copy-start.1
  55.4 0.0 copy-start
  55.4 13.0 %all-to-all-start = ((bf16[128,4,4,16,128]{4,3,2,1,0:T(8,128)(2,1)}), bf16[128,4,4,16,128]{4,3,2,1,0:T(8,128)(2,1)}, u32[]{:S(2)}, u32[]{:S(2)}) async-start(bf16[128,4,4,16,128]{4,3,2,1,0:T(8,128)(2,1)} %shard_map.82), calls=%async_computation | async-start | bytes 16777216 | tf_op jit(solution)/shard_map/all_to_all | solution.py:357
  68.4 0.0 copy-done.2
  68.4 0.2 reshape.18
  68.6 0.2 copy.12
  68.9 0.2 reshape.19
  69.0 0.1 copy.14.weight
  69.1 0.0 copy-done.1
  69.1 0.2 reshape.20
  69.3 0.2 copy.13
  69.5 0.2 reshape.21
  69.7 0.1 copy.15.power
  69.8 97.5 %all-to-all-done.spectra = bf16[128,4,4,16,128]{4,3,2,1,0:T(8,128)(2,1)} async-done(((bf16[128,4,4,16,128]{4,3,2,1,0:T(8,128)(2,1)}), bf16[128,4,4,16,128]{4,3,2,1,0:T(8,128)(2,1)}, u32[]{:S(2)}, u32[]{:S(2)}) %all-to-all-start) | async-done | bytes 8388640 | tf_op jit(solution)/shard_map/all_to_all | solution.py:357
  167.3 0.0 copy-done
  167.3 60.0 %shard_map.83 = f32[2,128,128]{2,1,0:T(8,128)S(1)} custom-call(bf16[128,4,4,16,128]{4,3,2,1,0:T(8,128)(2,1)} %all-to-all-done.spectra, f32[128,128]{1,0:T(8,128)S(1)} %copy.14.weight, f32[128,128]{1,0:T(8,128)S(1)} %copy.15.power, f32[128,128]{1,0:T(8,128)S(1)} %copy-done), custom_call_target="tpu_custom_call" | custom-call | flops 10000000000 | bytes 20000000 | tf_op jit(solution)/shard_map/pallas_call | solution.py:331
  227.3 0.1 copy.16
  227.4 0.3 reshape.22
  227.7 0.4 copy.17
  228.0 1.3 reshape.23
  (1 shorter events, 0.0 us)
Async XLA Ops:
  1.2 20.1 %collective-permute-start = (bf16[2,16,12288]{2,1,0:T(8,128)(2,1)S(1)}, bf16[2,16,12288]{2,1,0:T(8,128)(2,1)S(1)}, u32[]{:S(2)}, u32[]{:S(2)}) collective-permute-start(bf16[2,16,12288]{2,1,0:T(8,128)(2,1)S(1)} %slice.3), channel_id=1, source_target_pairs={{0,32},{32,64},{64,96},{1,33},{33,65},{65,97},{2,34},{34,66},{66,9... | collective-permute-start | bytes 2359304 | tf_op jit(solution)/shard_map/ppermute | solution.py:355
  21.3 0.9 copy-start.3
  55.4 13.0 %copy-start.2 = (s32[32,512]{1,0:T(8,128)S(1)}, s32[32,512]{1,0:T(8,128)}, u32[]{:S(2)}) copy-start(s32[32,512]{1,0:T(8,128)} %param.9) | copy-start | bytes 196612
  55.4 13.7 %copy-start.1 = (f32[32,512]{1,0:T(8,128)S(1)}, f32[32,512]{1,0:T(8,128)}, u32[]{:S(2)}) copy-start(f32[32,512]{1,0:T(8,128)} %param.10) | copy-start | bytes 196612
  55.4 111.9 %copy-start = (f32[128,128]{1,0:T(8,128)S(1)}, f32[128,128]{1,0:T(8,128)}, u32[]{:S(2)}) copy-start(f32[128,128]{1,0:T(8,128)} %constant.14.clone.share) | copy-start | bytes 196612
  55.4 111.9 %all-to-all-start = ((bf16[128,4,4,16,128]{4,3,2,1,0:T(8,128)(2,1)}), bf16[128,4,4,16,128]{4,3,2,1,0:T(8,128)(2,1)}, u32[]{:S(2)}, u32[]{:S(2)}) async-start(bf16[128,4,4,16,128]{4,3,2,1,0:T(8,128)(2,1)} %shard_map.82), calls=%async_computation | async-start | bytes 16777216 | tf_op jit(solution)/shard_map/all_to_all | solution.py:357

commit v2 on v1

v2 whole, which is shorter than its diff:
```python
import functools
import math

import jax
import jax.numpy as jnp
import numpy as np
from jax import lax
from jax.experimental import pallas as pl
from jax.experimental.pallas import tpu as pltpu
from jax.sharding import PartitionSpec as P

CHANNELS = 4096
TAPS = 4
ITERS = 5
EPSILON = 1e-06

COARSE = 32
FINE = 128
FEEDS_HERE = 16
BLOCKS_HERE = 32
GROUP = 8
GROUPS = BLOCKS_HERE // GROUP
PACKS = 4
OWNERS = 128
SECTIONS = 4
FEED_SETS = 32
SLOTS = SECTIONS * GROUPS
STEP = 45
STRIDE = 17
MARGIN = (TAPS - 1) * CHANNELS
LENGTH = BLOCKS_HERE * CHANNELS


def tables():
    position = np.arange(TAPS * CHANNELS, dtype=np.float64)
    offset = (position - 0.5 * TAPS * CHANNELS + 0.5) / CHANNELS
    window = 0.5 - 0.5 * np.cos(2.0 * np.pi * (position + 0.5) / (TAPS * CHANNELS))
    taps = np.sin(np.pi * offset) / (np.pi * offset) * window
    taps = taps.reshape(TAPS * COARSE, FINE).astype(np.float32)
    angle = 2.0 * np.pi * np.outer(np.arange(COARSE), np.arange(FINE)) / CHANNELS
    twiddle = np.concatenate([np.cos(angle), np.sin(angle)], axis=0).astype(np.float32)
    angle = 2.0 * np.pi * (np.outer(np.arange(FINE), np.arange(FINE)) % FINE) / FINE
    cosine = np.cos(angle) / math.sqrt(CHANNELS)
    sine = np.sin(angle) / math.sqrt(CHANNELS)
    fine = np.block([[cosine, sine], [-sine, cosine]]).astype(np.float32)
    lane = np.arange(128)
    share = (lane[:, None] // FEEDS_HERE == lane[None, :] // FEEDS_HERE).astype(np.float32)
    return taps, twiddle, fine, share


def butterfly_4(x):
    (ar, ai), (br, bi), (cr, ci), (dr, di) = x
    pr, pi, qr, qi = ar + cr, ai + ci, ar - cr, ai - ci
    sr, si, tr, ti = br + dr, bi + di, br - dr, bi - di
    return [(pr + sr, pi + si), (qr + ti, qi - tr), (pr - sr, pi - si), (qr - ti, qi + tr)]


def turn(x, eighths_of_32):
    n = eighths_of_32 % 32
    re, im = x
    if n == 0:
        return re, im
    if n == 8:
        return im, -re
    if n == 16:
        return -re, -im
    if n == 24:
        return -im, re
    cosine, sine = math.cos(2 * math.pi * n / 32), math.sin(2 * math.pi * n / 32)
    if n % 4 == 0:
        h = math.sqrt(0.5)
        if n == 4:
            return (re + im) * h, (im - re) * h
        if n == 12:
            return (im - re) * h, (re + im) * -h
    return re * cosine + im * sine, im * cosine - re * sine


def butterfly_8(x):
    even = butterfly_4([x[0], x[2], x[4], x[6]])
    odd = butterfly_4([x[1], x[3], x[5], x[7]])
    low, high = [], []
    for k in range(4):
        er, ei = even[k]
        tr, ti = turn(odd[k], 4 * k)
        low.append((er + tr, ei + ti))
        high.append((er - tr, ei - ti))
    return low + high


def first_transform(block, ext, taps, halfway):
    start = block * CHANNELS
    for low in range(8):
        points = []
        for high in range(4):
            tile = 8 * high + low
            pair = []
            for part in range(2):
                total = None
                for tap in range(TAPS):
                    at = pl.multiple_of(start + (tap * COARSE + tile) * FINE, FINE)
                    row = tap * COARSE + tile
                    term = taps[row : row + 1, :] * ext[part, :, pl.ds(at, FINE)].astype(jnp.float32)
                    total = term if total is None else total + term
                pair.append(total)
            points.append(tuple(pair))
        for q, point in enumerate(butterfly_4(points)):
            re, im = turn(point, low * q)
            halfway[q, low, 0] = re
            halfway[q, low, 1] = im


def second_transform(twiddle, halfway, upper, lower):
    for q1 in range(4):
        points = [(halfway[q1, low, 0], halfway[q1, low, 1]) for low in range(8)]
        for q2, (re, im) in enumerate(butterfly_8(points)):
            q = q1 + 4 * q2
            if q > 0:
                cosine = twiddle[q : q + 1, :]
                sine = twiddle[COARSE + q : COARSE + q + 1, :]
                re, im = re * cosine + im * sine, im * cosine - re * sine
            for part, value in enumerate((re, im)):
                high = value.astype(jnp.bfloat16)
                low = (value - high.astype(jnp.float32)).astype(jnp.bfloat16)
                rows = slice(q * FEEDS_HERE, (q + 1) * FEEDS_HERE)
                lanes = slice(part * FINE, (part + 1) * FINE)
                upper[rows, lanes] = high
                lower[rows, lanes] = low


def fine_transform(at, fine_upper, fine_lower, upper, lower, stage):
    dims = (((1,), (1,)), ((), ()))
    for half in range(2):
        rows = slice(half * 256, (half + 1) * 256)
        high = upper[rows, :]
        low = lower[rows, :]
        out = lax.dot_general(fine_upper[...], high, dims, preferred_element_type=jnp.float32)
        out += lax.dot_general(fine_lower[...], high, dims, preferred_element_type=jnp.float32)
        out += lax.dot_general(fine_upper[...], low, dims, preferred_element_type=jnp.float32)
        for pack in range(2):
            for part in range(2):
                piece = out[part * FINE : (part + 1) * FINE, pack * 128 : (pack + 1) * 128]
                stage[2 * half + pack, pl.ds(part * GROUP + at, OWNERS, stride=STRIDE), :] = piece


def copy_at(source, target, sems, at, peer):
    return pltpu.make_async_remote_copy(
        src_ref=source,
        dst_ref=target,
        send_sem=sems[0].at[at],
        recv_sem=sems[1].at[at],
        device_id=(lax.div(peer, FEED_SETS), lax.rem(peer, FEED_SETS)),
        device_id_type=pl.DeviceIdType.MESH,
    )


def exact_dot(left, right, split_left):
    value = left if split_left else right
    high = value.astype(jnp.bfloat16)
    low = (value - high.astype(jnp.float32)).astype(jnp.bfloat16)
    if split_left:
        return jnp.dot(high, right, preferred_element_type=jnp.float32) + jnp.dot(
            low, right, preferred_element_type=jnp.float32
        )
    return jnp.dot(left, high, preferred_element_type=jnp.float32) + jnp.dot(
        left, low, preferred_element_type=jnp.float32
    )


def solve_packs(tile, first, count, weight, power, share, x, coeff, fold, diag):
    feeds = FEED_SETS * 8
    own = pl.ds(pl.multiple_of(first * FEED_SETS, FEED_SETS), count * FEED_SETS)
    column = lax.broadcasted_iota(jnp.int32, (FEED_SETS, feeds), 1)
    row = lax.broadcasted_iota(jnp.int32, (FEED_SETS, feeds), 0)
    near = (column >= row * 8) & (column < row * 8 + 8)
    pick = jnp.where(near, 1.0, 0.0).astype(jnp.bfloat16)

    def diagonal(feed_set, carry):
        for pack in range(count):
            total = [jnp.zeros((GROUP, 128), jnp.float32) for _ in range(2)]
            for slot in range(SLOTS):
                re, im = tile(pack, slot, feed_set)
                total[0] = total[0] + re * re
                total[1] = total[1] + im * im
            fold[pack, 0, pl.ds(pl.multiple_of(feed_set * 8, 8), 8), :] = total[0] + total[1]
        return carry

    lax.fori_loop(0, FEED_SETS, diagonal, 0)
    w_all = weight[own, :]
    p_all = power[own, :]
    for pack in range(count):
        here = slice(pack * FEED_SETS, (pack + 1) * FEED_SETS)
        total = exact_dot(pick, fold[pack, 0], False)
        diag[here, :] = float(SLOTS * GROUP) * p_all[here] - total
    x[0, 0 : count * FEED_SETS, :] = w_all
    x[1, 0 : count * FEED_SETS, :] = jnp.zeros_like(w_all)

    def iterate(iteration, carry):
        for pack in range(count):

            def forward(index, inner):
                pr = [jnp.zeros((GROUP, 128), jnp.float32) for _ in range(4)]
                pi = [jnp.zeros((GROUP, 128), jnp.float32) for _ in range(4)]
                for feed_set in range(FEED_SETS):
                    at = pack * FEED_SETS + feed_set
                    xr = x[0, at : at + 1, :]
                    xi = x[1, at : at + 1, :]
                    for two in range(2):
                        re, im = tile(pack, index * 2 + two, feed_set)
                        pr[two] = pr[two] + re * xr
                        pr[2 + two] = pr[2 + two] + im * xi
                        pi[two] = pi[two] + re * xi
                        pi[2 + two] = pi[2 + two] - im * xr
                at = pl.multiple_of((pack * SLOTS + index * 2) * GROUP, 2 * GROUP)
                for two in range(2):
                    coeff[0, pl.ds(at + two * GROUP, GROUP), :] = pr[two] + pr[2 + two]
                    coeff[1, pl.ds(at + two * GROUP, GROUP), :] = pi[two] + pi[2 + two]
                return inner

            lax.fori_loop(0, SLOTS // 2, forward, 0)
        for part in range(2):
            rows = slice(0, count * SLOTS * GROUP)
            coeff[part, rows, :] = exact_dot(coeff[part, rows, :], share[...], True)

        for pack in range(count):

            def backward(index, inner):
                yr = [jnp.zeros((GROUP, 128), jnp.float32) for _ in range(8)]
                yi = [jnp.zeros((GROUP, 128), jnp.float32) for _ in range(8)]
                for slot in range(SLOTS):
                    at = (pack * SLOTS + slot) * GROUP
                    pr = coeff[0, at : at + GROUP, :]
                    pi = coeff[1, at : at + GROUP, :]
                    for two in range(4):
                        re, im = tile(pack, slot, index * 4 + two)
                        yr[two] = yr[two] + re * pr
                        yr[4 + two] = yr[4 + two] - im * pi
                        yi[two] = yi[two] + re * pi
                        yi[4 + two] = yi[4 + two] + im * pr
                for two in range(4):
                    at = pl.multiple_of((index * 4 + two) * 8, 8)
                    fold[pack, 0, pl.ds(at, 8), :] = yr[two] + yr[4 + two]
                    fold[pack, 1, pl.ds(at, 8), :] = yi[two] + yi[4 + two]
                return inner

            lax.fori_loop(0, FEED_SETS // 4, backward, 0)
        for pack in range(count):
            here = slice(pack * FEED_SETS, (pack + 1) * FEED_SETS)
            w = w_all[here]
            squares = jnp.zeros((1, 128), jnp.float32)
            parts = []
            for part in range(2):
                total = exact_dot(pick, fold[pack, part], False)
                value = w * (total + diag[here, :] * (w * x[part, here, :]))
                parts.append(value)
                squares = squares + jnp.sum(value * value, axis=0, keepdims=True)
            squares = jnp.broadcast_to(squares, (8, 128))
            total = jnp.dot(
                squares,
                share[...].astype(jnp.float32),
                precision=lax.Precision.HIGHEST,
                preferred_element_type=jnp.float32,
            )
            length = jnp.sqrt(total[0:1] + EPSILON)
            scale = jnp.where(iteration == ITERS - 1, jnp.sqrt(length), length)
            for part in range(2):
                x[part, here, :] = parts[part] / scale
        return carry

    lax.fori_loop(0, ITERS, iterate, 0)


def kernel(
    volt, taps, twiddle, fine_upper, fine_lower, weight, power, share, out,
    ext, halfway, upper, lower, stage, sent_pair, sent_one, held_pair, held_one,
    x, coeff, fold, diag, loads, send_sems, recv_sems, edge_sems,
):
    section = lax.axis_index("section")
    me = section * FEED_SETS + lax.axis_index("chan")
    sems = (send_sems, recv_sems)
    barrier = pltpu.get_barrier_semaphore()

    def greet(step, carry):
        peer = lax.rem(me + lax.rem(step * STEP, OWNERS), OWNERS)
        pl.semaphore_signal(
            barrier,
            inc=1,
            device_id=(lax.div(peer, FEED_SETS), lax.rem(peer, FEED_SETS)),
            device_id_type=pl.DeviceIdType.MESH,
        )
        return carry

    lax.fori_loop(1, OWNERS, greet, 0)

    def load(group):
        width = GROUP * CHANNELS
        start = pl.multiple_of(group * width, width)
        return pltpu.make_async_copy(
            volt.at[:, :, pl.ds(start, width)],
            ext.at[:, :, pl.ds(MARGIN + start, width)],
            loads.at[group],
        )

    edge = pltpu.make_async_remote_copy(
        src_ref=volt.at[:, :, pl.ds(LENGTH - MARGIN, MARGIN)],
        dst_ref=ext.at[:, :, pl.ds(0, MARGIN)],
        send_sem=edge_sems.at[0],
        recv_sem=edge_sems.at[1],
        device_id=(lax.rem(section + 1, SECTIONS), lax.axis_index("chan")),
        device_id_type=pl.DeviceIdType.MESH,
    )
    for position in range(GROUPS):
        load((position) % GROUPS).start()
    load(0).wait()

    def grouped(position, carry):
        group = lax.rem(position + 1, GROUPS)

        @pl.when(position < GROUPS - 1)
        def _():
            load(group).wait()

        @pl.when(position == GROUPS - 1)
        def _():
            edge.wait()

            @pl.when(section == 0)
            def _():
                def clear(at, inner):
                    where = pl.ds(pl.multiple_of(at * FINE, FINE), FINE)
                    for part in range(2):
                        ext[part, :, where] = jnp.zeros((FEEDS_HERE, FINE), jnp.bfloat16)
                    return inner

                lax.fori_loop(0, MARGIN // FINE, clear, 0)

        def step(at, inner):
            first_transform(group * GROUP + at, ext, taps, halfway)
            second_transform(twiddle, halfway, upper, lower)
            fine_transform(at, fine_upper, fine_lower, upper, lower, stage)
            return inner

        lax.fori_loop(0, GROUP, step, 0)

        def emit(owner, inner):
            rows = pl.ds(owner * STRIDE, 16)
            for pack in range(2):
                sent_pair[owner, group, pack] = stage[pack, rows, :].astype(jnp.bfloat16)
                sent_one[pack, owner, group] = stage[2 + pack, rows, :].astype(jnp.bfloat16)
            return inner

        lax.fori_loop(0, OWNERS, emit, 0, unroll=8)

        @pl.when(position == 0)
        def _():
            pl.semaphore_wait(barrier, OWNERS - 1)
            edge.start()

        def send(step, inner):
            peer = lax.rem(me + lax.rem(step * STEP, OWNERS), OWNERS)
            copy_at(sent_pair.at[peer, group], held_pair.at[me, group], sems, 0, peer).start()
            return inner

        lax.fori_loop(1, OWNERS, send, 0)
        return carry

    lax.fori_loop(0, GROUPS, grouped, 0)
    for pack in range(2):

        def send(step, inner):
            peer = lax.rem(me + lax.rem(step * STEP, OWNERS), OWNERS)
            copy_at(
                sent_one.at[pack, peer], held_one.at[pack, me], sems, 1 + pack, peer
            ).start()
            return inner

        lax.fori_loop(1, OWNERS, send, 0)

    for group in range(GROUPS):
        for pack in range(2):
            held_pair[me, group, pack] = sent_pair[me, group, pack]
            held_one[pack, me, group] = sent_one[pack, me, group]

    others = pl.ds(0, OWNERS - 1)
    pltpu.make_async_copy(sent_pair.at[others], held_pair.at[others], recv_sems.at[0]).wait()

    def tile_pair(pack, slot, feed_set):
        source = lax.div(slot, GROUPS) * FEED_SETS + feed_set
        value = held_pair[source, lax.rem(slot, GROUPS), pack].astype(jnp.float32)
        return value[0:GROUP], value[GROUP:]

    solve_packs(tile_pair, 0, 2, weight, power, share, x, coeff, fold, diag)
    out[:, 0 : 2 * FEED_SETS, :] = x[...]

    def single(index, carry):
        pltpu.make_async_copy(
            sent_one.at[0, others], held_one.at[index, others], recv_sems.at[1 + index]
        ).wait()

        def tile_one(pack, slot, feed_set):
            source = lax.div(slot, GROUPS) * FEED_SETS + feed_set
            value = held_one[index, source, lax.rem(slot, GROUPS)].astype(jnp.float32)
            return value[0:GROUP], value[GROUP:]

        solve_packs(tile_one, 2 + index, 1, weight, power, share, x, coeff, fold, diag)
        at = pl.multiple_of((2 + index) * FEED_SETS, FEED_SETS)
        out[:, pl.ds(at, FEED_SETS), :] = x[:, 0:FEED_SETS, :]
        return carry

    lax.fori_loop(0, 2, single, 0)
    pltpu.make_async_copy(sent_pair.at[others], held_pair.at[others], send_sems.at[0]).wait()
    for pack in range(2):
        pltpu.make_async_copy(
            sent_one.at[pack, others], held_one.at[pack, others], send_sems.at[1 + pack]
        ).wait()


def local(voltages, usable, auto_power):
    taps, twiddle, fine, share = tables()
    upper = fine.astype(jnp.bfloat16)
    lower = (fine - upper.astype(np.float32)).astype(jnp.bfloat16)
    rows = PACKS * FEED_SETS

    def arrange(array):
        array = array.reshape(PACKS, 8, FEED_SETS, FEEDS_HERE)
        return array.transpose(0, 2, 1, 3).reshape(rows, 128)

    vmem = pl.BlockSpec(memory_space=pltpu.VMEM)
    pair = pltpu.VMEM((OWNERS, GROUPS, 2, 16, 128), jnp.bfloat16)
    one = pltpu.VMEM((2, OWNERS, GROUPS, 16, 128), jnp.bfloat16)
    gains = pl.pallas_call(
        kernel,
        out_shape=jax.ShapeDtypeStruct((2, rows, 128), jnp.float32),
        in_specs=[pl.BlockSpec(memory_space=pl.ANY)] + [vmem] * 7,
        out_specs=vmem,
        scratch_shapes=[
            pltpu.VMEM((2, FEEDS_HERE, MARGIN + LENGTH), jnp.bfloat16),
            pltpu.VMEM((4, 8, 2, FEEDS_HERE, FINE), jnp.float32),
            pltpu.VMEM((COARSE * FEEDS_HERE, 256), jnp.bfloat16),
            pltpu.VMEM((COARSE * FEEDS_HERE, 256), jnp.bfloat16),
            pltpu.VMEM((PACKS, OWNERS * STRIDE + 8, 128), jnp.float32),
            pair,
            one,
            pair,
            one,
            pltpu.VMEM((2, 2 * FEED_SETS, 128), jnp.float32),
            pltpu.VMEM((2, 2 * SLOTS * GROUP, 128), jnp.float32),
            pltpu.VMEM((2, 2, FEED_SETS * 8, 128), jnp.float32),
            pltpu.VMEM((2 * FEED_SETS, 128), jnp.float32),
            pltpu.SemaphoreType.DMA((GROUPS,)),
            pltpu.SemaphoreType.DMA((3,)),
            pltpu.SemaphoreType.DMA((3,)),
            pltpu.SemaphoreType.DMA((2,)),
        ],
        compiler_params=pltpu.CompilerParams(
            collective_id=0, has_side_effects=True, vmem_limit_bytes=56 * 1024 * 1024
        ),
        cost_estimate=pl.CostEstimate(flops=10**10, bytes_accessed=2 * 10**7, transcendentals=0),
    )(
        voltages, taps, twiddle, upper, lower,
        arrange(usable.astype(jnp.float32)), arrange(auto_power), share.astype(jnp.bfloat16),
    )
    gains = gains.reshape(2, PACKS, FEED_SETS, 8, FEEDS_HERE).transpose(0, 1, 3, 2, 4)
    return gains.reshape(2, PACKS * 8, FEED_SETS * FEEDS_HERE)


def solution(mesh):
    in_specs = (
        P(None, "chan", "section"),
        P(("section", "chan"), None),
        P(("section", "chan"), None),
    )
    out_specs = P(None, ("section", "chan"), None)
    return jax.shard_map(local, mesh=mesh, in_specs=in_specs, out_specs=out_specs, check_vma=False)
```

time: 234 us -> 148 us (0.63); the launches traced: 229 us -> 148 us
  waiting for transfers between devices: 114 us -> 0 us
  Pallas kernels: 93.1 us -> 141 us
  starting transfers between devices: 17 us -> 0 us
    all_to_all x1 -> x0, waiting for transfers between devices: 97.5 us -> none  [local(): lax.all_to_all(spectra, ('section', 'chan'), split_axis=0, concat_axis=0,...]
    pallas_call x2 -> x1, Pallas kernels: 93.1 us -> 141 us  [local(): pl.pallas_call(kernel, out_shape=jax.ShapeDtypeStruct((2, rows, 128), jnp...]
    ppermute x1 -> x0, waiting for transfers between devices: 16.2 us -> none  [local(): history = lax.ppermute(tail_samples, 'section', route)]
    all_to_all x1 -> x0, starting transfers between devices: 13 us -> none  [local(): lax.all_to_all(spectra, ('section', 'chan'), split_axis=0, concat_axis=0,...]
    ppermute x1 -> x0, starting transfers between devices: 3.98 us -> none  [local(): history = lax.ppermute(tail_samples, 'section', route)]
  transfers between devices with their start and end apart: 2 -> 0, of which waited for: 2 -> 0; matrix products, arithmetic and copies ran while one was open for 1% -> 0% of each run, Pallas kernels for 0% -> 0%
where the time goes in v2:
time: 148 us
  Pallas kernels  141 us (95%)
  local copies, waits for them, and re-layouts  6.34 us (4%)
    pallas_call x1, Pallas kernels, local(): pl.pallas_call(kernel, out_shape=jax.ShapeDtypeStruct((2, rows, 128), jnp...  141 us

profile of v2, /device:TPU:1, one launch (start us, length us, event | category | flops | bytes accessed | tf_op | source)
XLA Modules:
  0.0 148.0 jit_solution(10112511765172193970)
XLA Ops:
  0.0 0.8 convert_element_type.3
  0.8 0.2 reshape.18
  1.1 0.2 copy.12
  1.3 0.2 reshape.19
  1.4 0.7 copy.14.weight
  2.2 1.0 reshape.20
  3.2 0.2 copy.13
  3.4 0.2 reshape.21
  3.6 0.7 copy.15.power
  4.3 140.7 %shard_map.82 = f32[2,128,128]{2,1,0:T(8,128)} custom-call(bf16[2,16,131072]{2,1,0:T(8,128)(2,1)} %volt.1, f32[128,128]{1,0:T(8,128)} %constant.10.clone.taps, f32[64,128]{1,0:T(8,128)} %constant.11.clone.twiddle, bf16[256,256]{1,0:T(8,128)(2,1)} %constant.12.clone.fine_upper, bf16[256,256]{1,0:T(8,128)(2,1)} %constant.13.clone.fine_lower, ...), custom_call_target="tpu_custom_call" | custom-call | flops 10000000000 | bytes 20000000 | tf_op jit(solution)/shard_map/pallas_call | solution.py:431
  145.0 1.0 copy.16
  146.0 0.3 reshape.22
  146.3 0.4 copy.17
  146.7 1.3 reshape.23

commit v3 on v2

--- a/solution.py
+++ b/solution.py
@@ -25,10 +25,10 @@
 SECTIONS = 4
 FEED_SETS = 32
 SLOTS = SECTIONS * GROUPS
-STEP = 45
 STRIDE = 17
-MARGIN = (TAPS - 1) * CHANNELS
 LENGTH = BLOCKS_HERE * CHANNELS
+EARLY = 2 * CHANNELS
+LATE = CHANNELS
 
 
 def tables():
@@ -143,57 +143,61 @@
                 stage[2 * half + pack, pl.ds(part * GROUP + at, OWNERS, stride=STRIDE), :] = piece
 
 
-def copy_at(source, target, sems, at, peer):
+def partner(step, section, chan):
+    def bit(at):
+        return lax.rem(lax.div(step, 2**at), 2)
+
+    there = lax.rem(section + bit(0) * 2 + bit(3), SECTIONS)
+    y = lax.rem(lax.div(chan, 8) + bit(1) * 2 + bit(4), 4)
+    z = lax.rem(lax.div(chan, 2) + bit(2) * 2 + bit(5), 4)
+    core = lax.rem(chan + bit(6), 2)
+    return there, y * 8 + z * 2 + core
+
+
+def copy_at(source, target, sems, at, device):
     return pltpu.make_async_remote_copy(
         src_ref=source,
         dst_ref=target,
         send_sem=sems[0].at[at],
         recv_sem=sems[1].at[at],
-        device_id=(lax.div(peer, FEED_SETS), lax.rem(peer, FEED_SETS)),
+        device_id=device,
         device_id_type=pl.DeviceIdType.MESH,
     )
 
 
-def exact_dot(left, right, split_left):
-    value = left if split_left else right
+def share_dot(value, share):
     high = value.astype(jnp.bfloat16)
     low = (value - high.astype(jnp.float32)).astype(jnp.bfloat16)
-    if split_left:
-        return jnp.dot(high, right, preferred_element_type=jnp.float32) + jnp.dot(
-            low, right, preferred_element_type=jnp.float32
-        )
-    return jnp.dot(left, high, preferred_element_type=jnp.float32) + jnp.dot(
-        left, low, preferred_element_type=jnp.float32
-    )
-
-
-def solve_packs(tile, first, count, weight, power, share, x, coeff, fold, diag):
-    feeds = FEED_SETS * 8
+    total = jnp.dot(high, share, preferred_element_type=jnp.float32)
+    return total + jnp.dot(low, share, preferred_element_type=jnp.float32)
+
+
+def solve_packs(tile, first, count, weight, power, share, x, y, coeff, squares, diag):
     own = pl.ds(pl.multiple_of(first * FEED_SETS, FEED_SETS), count * FEED_SETS)
-    column = lax.broadcasted_iota(jnp.int32, (FEED_SETS, feeds), 1)
-    row = lax.broadcasted_iota(jnp.int32, (FEED_SETS, feeds), 0)
-    near = (column >= row * 8) & (column < row * 8 + 8)
-    pick = jnp.where(near, 1.0, 0.0).astype(jnp.bfloat16)
 
     def diagonal(feed_set, carry):
         for pack in range(count):
-            total = [jnp.zeros((GROUP, 128), jnp.float32) for _ in range(2)]
+            total = [jnp.zeros((GROUP, 128), jnp.float32) for _ in range(4)]
             for slot in range(SLOTS):
                 re, im = tile(pack, slot, feed_set)
-                total[0] = total[0] + re * re
-                total[1] = total[1] + im * im
-            fold[pack, 0, pl.ds(pl.multiple_of(feed_set * 8, 8), 8), :] = total[0] + total[1]
+                at = slot % 2
+                total[at] = total[at] + re * re
+                total[2 + at] = total[2 + at] + im * im
+            total = (total[0] + total[1]) + (total[2] + total[3])
+            at = pl.ds(pack * FEED_SETS + feed_set, 1)
+            diag[at, :] = jnp.sum(total, axis=0, keepdims=True)
         return carry
 
     lax.fori_loop(0, FEED_SETS, diagonal, 0)
-    w_all = weight[own, :]
-    p_all = power[own, :]
-    for pack in range(count):
-        here = slice(pack * FEED_SETS, (pack + 1) * FEED_SETS)
-        total = exact_dot(pick, fold[pack, 0], False)
-        diag[here, :] = float(SLOTS * GROUP) * p_all[here] - total
-    x[0, 0 : count * FEED_SETS, :] = w_all
-    x[1, 0 : count * FEED_SETS, :] = jnp.zeros_like(w_all)
+    span = slice(0, count * FEED_SETS)
+    diag[span, :] = float(SLOTS * GROUP) * power[own, :] - diag[span, :]
+    x[0, span, :] = weight[own, :]
+    x[1, span, :] = jnp.zeros((count * FEED_SETS, 128), jnp.float32)
+    squares[...] = jnp.zeros_like(squares)
+
+    def lengths():
+        total = share_dot(squares[...], share[...])
+        return [jnp.sqrt(total[8 * pack : 8 * pack + 1] + EPSILON) for pack in range(count)]
 
     def iterate(iteration, carry):
         for pack in range(count):
@@ -218,10 +222,11 @@
                 return inner
 
             lax.fori_loop(0, SLOTS // 2, forward, 0)
-        for part in range(2):
-            rows = slice(0, count * SLOTS * GROUP)
-            coeff[part, rows, :] = exact_dot(coeff[part, rows, :], share[...], True)
-
+        inverse = [jnp.where(iteration == 0, 1.0, 1.0 / length) for length in lengths()]
+        for pack in range(count):
+            rows = slice(pack * SLOTS * GROUP, (pack + 1) * SLOTS * GROUP)
+            for part in range(2):
+                coeff[part, rows, :] = share_dot(coeff[part, rows, :], share[...]) * inverse[pack]
         for pack in range(count):
 
             def backward(index, inner):
@@ -238,103 +243,136 @@
                         yi[two] = yi[two] + re * pi
                         yi[4 + two] = yi[4 + two] + im * pr
                 for two in range(4):
-                    at = pl.multiple_of((index * 4 + two) * 8, 8)
-                    fold[pack, 0, pl.ds(at, 8), :] = yr[two] + yr[4 + two]
-                    fold[pack, 1, pl.ds(at, 8), :] = yi[two] + yi[4 + two]
+                    at = pl.ds(pack * FEED_SETS + index * 4 + two, 1)
+                    y[0, at, :] = jnp.sum(yr[two] + yr[4 + two], axis=0, keepdims=True)
+                    y[1, at, :] = jnp.sum(yi[two] + yi[4 + two], axis=0, keepdims=True)
                 return inner
 
             lax.fori_loop(0, FEED_SETS // 4, backward, 0)
         for pack in range(count):
             here = slice(pack * FEED_SETS, (pack + 1) * FEED_SETS)
-            w = w_all[here]
-            squares = jnp.zeros((1, 128), jnp.float32)
-            parts = []
+            at = pl.ds(pl.multiple_of((first + pack) * FEED_SETS, FEED_SETS), FEED_SETS)
+            w = weight[at, :]
+            scaled = w * (diag[here, :] * (w * inverse[pack]))
+            total = jnp.zeros((8, 128), jnp.float32)
             for part in range(2):
-                total = exact_dot(pick, fold[pack, part], False)
-                value = w * (total + diag[here, :] * (w * x[part, here, :]))
-                parts.append(value)
-                squares = squares + jnp.sum(value * value, axis=0, keepdims=True)
-            squares = jnp.broadcast_to(squares, (8, 128))
-            total = jnp.dot(
-                squares,
-                share[...].astype(jnp.float32),
-                precision=lax.Precision.HIGHEST,
-                preferred_element_type=jnp.float32,
-            )
-            length = jnp.sqrt(total[0:1] + EPSILON)
-            scale = jnp.where(iteration == ITERS - 1, jnp.sqrt(length), length)
-            for part in range(2):
-                x[part, here, :] = parts[part] / scale
+                value = w * y[part, here, :] + scaled * x[part, here, :]
+                x[part, here, :] = value
+                for row in range(0, FEED_SETS, 8):
+                    total = total + value[row : row + 8] * value[row : row + 8]
+            total = jnp.sum(total, axis=0, keepdims=True)
+            squares[8 * pack : 8 * pack + 8, :] = jnp.broadcast_to(total, (8, 128))
         return carry
 
     lax.fori_loop(0, ITERS, iterate, 0)
+    for pack, length in enumerate(lengths()):
+        here = slice(pack * FEED_SETS, (pack + 1) * FEED_SETS)
+        for part in range(2):
+            x[part, here, :] = x[part, here, :] / jnp.sqrt(length)
 
 
 def kernel(
-    volt, taps, twiddle, fine_upper, fine_lower, weight, power, share, out,
-    ext, halfway, upper, lower, stage, sent_pair, sent_one, held_pair, held_one,
-    x, coeff, fold, diag, loads, send_sems, recv_sems, edge_sems,
+    volt, taps, twiddle, fine_upper, fine_lower, usable, auto_power, share, repeat, out,
+    weight, power, lined, ext, halfway, upper, lower, stage, sent_pair, sent_one, held_pair, held_one,
+    x, y, coeff, squares, diag, loads, send_sems, recv_sems, edge_sems,
 ):
+    def arrange(source, target, split):
+        feeds = FEED_SETS * FEEDS_HERE
+        lane = lax.broadcasted_iota(jnp.int32, (FEED_SETS, feeds), 1)
+        first = lax.broadcasted_iota(jnp.int32, (FEED_SETS, feeds), 0) * FEEDS_HERE
+        mine = (lane >= first) & (lane < first + FEEDS_HERE)
+        place = lax.broadcasted_iota(jnp.int32, (FEED_SETS, 128), 1)
+
+        def body(pack, carry):
+            for q in range(8):
+                row = source[pl.ds(pack * 8 + q, 1), :].astype(jnp.float32)
+                lined[q * FEED_SETS : (q + 1) * FEED_SETS, :] = jnp.where(mine, row, 0.0)
+            value = lined[...]
+            high = value.astype(jnp.bfloat16)
+            wide = jnp.dot(high, repeat[...], preferred_element_type=jnp.float32)
+            if split:
+                rest = value - high.astype(jnp.float32)
+                middle = rest.astype(jnp.bfloat16)
+                low = (rest - middle.astype(jnp.float32)).astype(jnp.bfloat16)
+                wide = wide + jnp.dot(middle, repeat[...], preferred_element_type=jnp.float32)
+                wide = wide + jnp.dot(low, repeat[...], preferred_element_type=jnp.float32)
+            total = jnp.zeros((FEED_SETS, 128), jnp.float32)
+            for q in range(8):
+                part = wide[q * FEED_SETS : (q + 1) * FEED_SETS]
+                own = (place >= q * FEEDS_HERE) & (place < (q + 1) * FEEDS_HERE)
+                total = total + jnp.where(own, part, 0.0)
+            target[pl.ds(pl.multiple_of(pack * FEED_SETS, FEED_SETS), FEED_SETS), :] = total
+            return carry
+
+        lax.fori_loop(0, PACKS, body, 0)
+
     section = lax.axis_index("section")
-    me = section * FEED_SETS + lax.axis_index("chan")
+    chan = lax.axis_index("chan")
+    me = section * FEED_SETS + chan
     sems = (send_sems, recv_sems)
+    load = pltpu.make_async_copy(volt, ext.at[:, :, pl.ds(EARLY, LENGTH)], loads)
+    load.start()
     barrier = pltpu.get_barrier_semaphore()
 
     def greet(step, carry):
-        peer = lax.rem(me + lax.rem(step * STEP, OWNERS), OWNERS)
         pl.semaphore_signal(
             barrier,
             inc=1,
-            device_id=(lax.div(peer, FEED_SETS), lax.rem(peer, FEED_SETS)),
+            device_id=partner(step, section, chan),
             device_id_type=pl.DeviceIdType.MESH,
         )
         return carry
 
     lax.fori_loop(1, OWNERS, greet, 0)
-
-    def load(group):
-        width = GROUP * CHANNELS
-        start = pl.multiple_of(group * width, width)
-        return pltpu.make_async_copy(
-            volt.at[:, :, pl.ds(start, width)],
-            ext.at[:, :, pl.ds(MARGIN + start, width)],
-            loads.at[group],
-        )
-
-    edge = pltpu.make_async_remote_copy(
-        src_ref=volt.at[:, :, pl.ds(LENGTH - MARGIN, MARGIN)],
-        dst_ref=ext.at[:, :, pl.ds(0, MARGIN)],
-        send_sem=edge_sems.at[0],
-        recv_sem=edge_sems.at[1],
-        device_id=(lax.rem(section + 1, SECTIONS), lax.axis_index("chan")),
-        device_id_type=pl.DeviceIdType.MESH,
+    early = copy_at(
+        volt.at[:, :, pl.ds(LENGTH - EARLY, EARLY)],
+        ext.at[:, :, pl.ds(0, EARLY)],
+        (edge_sems, edge_sems.at[pl.ds(2, 2)]),
+        0,
+        (lax.rem(section + 1, SECTIONS), chan),
     )
-    for position in range(GROUPS):
-        load((position) % GROUPS).start()
-    load(0).wait()
+    late = copy_at(
+        volt.at[:, :, pl.ds(0, LATE)],
+        ext.at[:, :, pl.ds(EARLY + LENGTH, LATE)],
+        (edge_sems, edge_sems.at[pl.ds(2, 2)]),
+        1,
+        (lax.rem(section + SECTIONS - 1, SECTIONS), chan),
+    )
+    pl.semaphore_wait(barrier, OWNERS - 1)
+    early.start()
+    late.start()
+    arrange(usable, weight, False)
+    load.wait()
+
+    def clear(first, count):
+        def body(at, inner):
+            where = pl.ds(pl.multiple_of(first * CHANNELS + at * FINE, FINE), FINE)
+            for part in range(2):
+                ext[part, :, where] = jnp.zeros((FEEDS_HERE, FINE), jnp.bfloat16)
+            return inner
+
+        lax.fori_loop(0, count * COARSE, body, 0)
 
     def grouped(position, carry):
         group = lax.rem(position + 1, GROUPS)
 
-        @pl.when(position < GROUPS - 1)
+        @pl.when(position == 2)
         def _():
-            load(group).wait()
-
-        @pl.when(position == GROUPS - 1)
+            late.wait()
+
+        @pl.when(position == 3)
         def _():
-            edge.wait()
+            early.wait()
 
             @pl.when(section == 0)
             def _():
-                def clear(at, inner):
-                    where = pl.ds(pl.multiple_of(at * FINE, FINE), FINE)
-                    for part in range(2):
-                        ext[part, :, where] = jnp.zeros((FEEDS_HERE, FINE), jnp.bfloat16)
-                    return inner
-
-                lax.fori_loop(0, MARGIN // FINE, clear, 0)
+                clear(0, 2)
 
         def step(at, inner):
+            @pl.when((section == SECTIONS - 1) & (position == 2) & (at == GROUP - 1))
+            def _():
+                clear(BLOCKS_HERE - 1, TAPS - 1)
+
             first_transform(group * GROUP + at, ext, taps, halfway)
             second_transform(twiddle, halfway, upper, lower)
             fine_transform(at, fine_upper, fine_lower, upper, lower, stage)
@@ -351,30 +389,29 @@
 
         lax.fori_loop(0, OWNERS, emit, 0, unroll=8)
 
-        @pl.when(position == 0)
-        def _():
-            pl.semaphore_wait(barrier, OWNERS - 1)
-            edge.start()
-
         def send(step, inner):
-            peer = lax.rem(me + lax.rem(step * STEP, OWNERS), OWNERS)
-            copy_at(sent_pair.at[peer, group], held_pair.at[me, group], sems, 0, peer).start()
+            there, column = partner(step, section, chan)
+            source = sent_pair.at[there * FEED_SETS + column, group]
+            copy_at(source, held_pair.at[me, group], sems, 0, (there, column)).start()
             return inner
 
         lax.fori_loop(1, OWNERS, send, 0)
         return carry
 
     lax.fori_loop(0, GROUPS, grouped, 0)
-    for pack in range(2):
-
+
+    def rest(pack, carry):
         def send(step, inner):
-            peer = lax.rem(me + lax.rem(step * STEP, OWNERS), OWNERS)
-            copy_at(
-                sent_one.at[pack, peer], held_one.at[pack, me], sems, 1 + pack, peer
-            ).start()
+            there, column = partner(step, section, chan)
+            source = sent_one.at[pack, there * FEED_SETS + column]
+            copy_at(source, held_one.at[pack, me], sems, 1 + pack, (there, column)).start()
             return inner
 
         lax.fori_loop(1, OWNERS, send, 0)
+        return carry
+
+    lax.fori_loop(0, 2, rest, 0)
+    arrange(auto_power, power, True)
 
     for group in range(GROUPS):
         for pack in range(2):
@@ -389,7 +426,7 @@
         value = held_pair[source, lax.rem(slot, GROUPS), pack].astype(jnp.float32)
         return value[0:GROUP], value[GROUP:]
 
-    solve_packs(tile_pair, 0, 2, weight, power, share, x, coeff, fold, diag)
+    solve_packs(tile_pair, 0, 2, weight, power, share, x, y, coeff, squares, diag)
     out[:, 0 : 2 * FEED_SETS, :] = x[...]
 
     def single(index, carry):
@@ -402,7 +439,7 @@
             value = held_one[index, source, lax.rem(slot, GROUPS)].astype(jnp.float32)
             return value[0:GROUP], value[GROUP:]
 
-        solve_packs(tile_one, 2 + index, 1, weight, power, share, x, coeff, fold, diag)
+        solve_packs(tile_one, 2 + index, 1, weight, power, share, x, y, coeff, squares, diag)
         at = pl.multiple_of((2 + index) * FEED_SETS, FEED_SETS)
         out[:, pl.ds(at, FEED_SETS), :] = x[:, 0:FEED_SETS, :]
         return carry
@@ -421,20 +458,21 @@
     lower = (fine - upper.astype(np.float32)).astype(jnp.bfloat16)
     rows = PACKS * FEED_SETS
 
-    def arrange(array):
-        array = array.reshape(PACKS, 8, FEED_SETS, FEEDS_HERE)
-        return array.transpose(0, 2, 1, 3).reshape(rows, 128)
-
+    lane = np.arange(FEED_SETS * FEEDS_HERE)[:, None] % FEEDS_HERE
+    repeat = (lane == np.arange(128)[None, :] % FEEDS_HERE).astype(jnp.bfloat16)
     vmem = pl.BlockSpec(memory_space=pltpu.VMEM)
     pair = pltpu.VMEM((OWNERS, GROUPS, 2, 16, 128), jnp.bfloat16)
     one = pltpu.VMEM((2, OWNERS, GROUPS, 16, 128), jnp.bfloat16)
     gains = pl.pallas_call(
         kernel,
         out_shape=jax.ShapeDtypeStruct((2, rows, 128), jnp.float32),
-        in_specs=[pl.BlockSpec(memory_space=pl.ANY)] + [vmem] * 7,
+        in_specs=[pl.BlockSpec(memory_space=pl.ANY)] + [vmem] * 8,
         out_specs=vmem,
         scratch_shapes=[
-            pltpu.VMEM((2, FEEDS_HERE, MARGIN + LENGTH), jnp.bfloat16),
+            pltpu.VMEM((rows, 128), jnp.float32),
+            pltpu.VMEM((rows, 128), jnp.float32),
+            pltpu.VMEM((8 * FEED_SETS, FEED_SETS * FEEDS_HERE), jnp.float32),
+            pltpu.VMEM((2, FEEDS_HERE, EARLY + LENGTH + LATE), jnp.bfloat16),
             pltpu.VMEM((4, 8, 2, FEEDS_HERE, FINE), jnp.float32),
             pltpu.VMEM((COARSE * FEEDS_HERE, 256), jnp.bfloat16),
             pltpu.VMEM((COARSE * FEEDS_HERE, 256), jnp.bfloat16),
@@ -444,13 +482,14 @@
             pair,
             one,
             pltpu.VMEM((2, 2 * FEED_SETS, 128), jnp.float32),
+            pltpu.VMEM((2, 2 * FEED_SETS, 128), jnp.float32),
             pltpu.VMEM((2, 2 * SLOTS * GROUP, 128), jnp.float32),
-            pltpu.VMEM((2, 2, FEED_SETS * 8, 128), jnp.float32),
+            pltpu.VMEM((16, 128), jnp.float32),
             pltpu.VMEM((2 * FEED_SETS, 128), jnp.float32),
-            pltpu.SemaphoreType.DMA((GROUPS,)),
+            pltpu.SemaphoreType.DMA,
             pltpu.SemaphoreType.DMA((3,)),
             pltpu.SemaphoreType.DMA((3,)),
-            pltpu.SemaphoreType.DMA((2,)),
+            pltpu.SemaphoreType.DMA((4,)),
         ],
         compiler_params=pltpu.CompilerParams(
             collective_id=0, has_side_effects=True, vmem_limit_bytes=56 * 1024 * 1024
@@ -458,7 +497,7 @@
         cost_estimate=pl.CostEstimate(flops=10**10, bytes_accessed=2 * 10**7, transcendentals=0),
     )(
         voltages, taps, twiddle, upper, lower,
-        arrange(usable.astype(jnp.float32)), arrange(auto_power), share.astype(jnp.bfloat16),
+        usable, auto_power, share.astype(jnp.bfloat16), repeat,
     )
     gains = gains.reshape(2, PACKS, FEED_SETS, 8, FEEDS_HERE).transpose(0, 1, 3, 2, 4)
     return gains.reshape(2, PACKS * 8, FEED_SETS * FEEDS_HERE)

time: 148 us -> 145 us (0.980)
  local copies, waits for them, and re-layouts: 6.34 us -> 2.91 us
    reshape x6 -> x0, local copies, waits for them, and re-layouts: 3.02 us -> none  [the longest x4 1.77 us: arrange(): return array.transpose(0, 2, 1, 3).reshape(rows, 128)]
    pallas_call x1, Pallas kernels: 141 us -> 142 us  [local(): pl.pallas_call(kernel, out_shape=jax.ShapeDtypeStruct((2, rows, 128), jnp...]
where the time goes in v3:
time: 145 us
  Pallas kernels  142 us (98%)
  local copies, waits for them, and re-layouts  2.91 us (2%)
    pallas_call x1, Pallas kernels, local(): pl.pallas_call(kernel, out_shape=jax.ShapeDtypeStruct((2, rows, 128), jnp...  142 us

profile of v3, /device:TPU:1, one launch (start us, length us, event | category | flops | bytes accessed | tf_op | source)
XLA Modules:
  0.0 145.2 jit_solution(12843948690978282291)
XLA Ops:
  0.0 142.3 %shard_map.91 = f32[2,128,128]{2,1,0:T(8,128)} custom-call(bf16[2,16,131072]{2,1,0:T(8,128)(2,1)} %volt.1, f32[128,128]{1,0:T(8,128)} %constant.12.clone.taps, f32[64,128]{1,0:T(8,128)} %constant.13.clone.twiddle, bf16[256,256]{1,0:T(8,128)(2,1)} %constant.14.clone.fine_upper, bf16[256,256]{1,0:T(8,128)(2,1)} %constant.15.clone.fine_lower, ...), custom_call_target="tpu_custom_call" | custom-call | flops 10000000000 | bytes 20000000 | tf_op jit(solution)/shard_map/pallas_call | solution.py:466
  142.3 1.0 copy.11
  143.3 0.3 reshape.6
  143.6 0.4 copy.12
  143.9 1.3 reshape.7

commit v4 on v3

--- a/solution.py
+++ b/solution.py
@@ -143,15 +143,29 @@
                 stage[2 * half + pack, pl.ds(part * GROUP + at, OWNERS, stride=STRIDE), :] = piece
 
 
-def partner(step, section, chan):
-    def bit(at):
-        return lax.rem(lax.div(step, 2**at), 2)
-
-    there = lax.rem(section + bit(0) * 2 + bit(3), SECTIONS)
-    y = lax.rem(lax.div(chan, 8) + bit(1) * 2 + bit(4), 4)
-    z = lax.rem(lax.div(chan, 2) + bit(2) * 2 + bit(5), 4)
-    core = lax.rem(chan + bit(6), 2)
-    return there, y * 8 + z * 2 + core
+def visit(section, chan, action):
+    row, column = lax.div(chan, 8), lax.rem(lax.div(chan, 2), 4)
+
+    def turns(near, core):
+        x = [lax.rem(section + near[0] + 2 * far, SECTIONS) for far in range(2)]
+        y = [lax.rem(row + near[1] + 2 * far, 4) * 8 for far in range(2)]
+        z = [lax.rem(column + near[2] + 2 * far, 4) * 2 + core for far in range(2)]
+        return x, y, z
+
+    def several(x, y, z, skip):
+        for step in range(skip, 8):
+            action(x[step % 2], y[step // 2 % 2] + z[step // 4])
+
+    same = lax.rem(chan, 2)
+    several(*turns((0, 0, 0), same), 1)
+
+    def body(step, carry):
+        near = [lax.rem(step, 2), lax.rem(lax.div(step, 2), 2), lax.rem(lax.div(step, 4), 2)]
+        core = lax.rem(same + lax.div(step, 8), 2)
+        several(*turns(near, core), 0)
+        return carry
+
+    lax.fori_loop(1, 16, body, 0)
 
 
 def copy_at(source, target, sems, at, device):
@@ -314,16 +328,12 @@
     load.start()
     barrier = pltpu.get_barrier_semaphore()
 
-    def greet(step, carry):
+    def greet(there, column):
         pl.semaphore_signal(
-            barrier,
-            inc=1,
-            device_id=partner(step, section, chan),
-            device_id_type=pl.DeviceIdType.MESH,
+            barrier, inc=1, device_id=(there, column), device_id_type=pl.DeviceIdType.MESH
         )
-        return carry
-
-    lax.fori_loop(1, OWNERS, greet, 0)
+
+    visit(section, chan, greet)
     early = copy_at(
         volt.at[:, :, pl.ds(LENGTH - EARLY, EARLY)],
         ext.at[:, :, pl.ds(0, EARLY)],
@@ -389,25 +399,21 @@
 
         lax.fori_loop(0, OWNERS, emit, 0, unroll=8)
 
-        def send(step, inner):
-            there, column = partner(step, section, chan)
+        def send(there, column):
             source = sent_pair.at[there * FEED_SETS + column, group]
             copy_at(source, held_pair.at[me, group], sems, 0, (there, column)).start()
-            return inner
-
-        lax.fori_loop(1, OWNERS, send, 0)
+
+        visit(section, chan, send)
         return carry
 
     lax.fori_loop(0, GROUPS, grouped, 0)
 
     def rest(pack, carry):
-        def send(step, inner):
-            there, column = partner(step, section, chan)
+        def send(there, column):
             source = sent_one.at[pack, there * FEED_SETS + column]
             copy_at(source, held_one.at[pack, me], sems, 1 + pack, (there, column)).start()
-            return inner
-
-        lax.fori_loop(1, OWNERS, send, 0)
+
+        visit(section, chan, send)
         return carry
 
     lax.fori_loop(0, 2, rest, 0)

time: 145 us -> 130 us (0.90)
  Pallas kernels: 142 us -> 127 us
    pallas_call x1, Pallas kernels: 142 us -> 127 us  [local(): pl.pallas_call(kernel, out_shape=jax.ShapeDtypeStruct((2, rows, 128), jnp...]
where the time goes in v4:
time: 130 us
  Pallas kernels  127 us (98%)
  local copies, waits for them, and re-layouts  2.91 us (2%)
    pallas_call x1, Pallas kernels, local(): pl.pallas_call(kernel, out_shape=jax.ShapeDtypeStruct((2, rows, 128), jnp...  127 us

profile of v4, /device:TPU:1, one launch (start us, length us, event | category | flops | bytes accessed | tf_op | source)
XLA Modules:
  0.0 130.2 jit_solution(14172414763072467338)
XLA Ops:
  0.0 127.2 %shard_map.91 = f32[2,128,128]{2,1,0:T(8,128)} custom-call(bf16[2,16,131072]{2,1,0:T(8,128)(2,1)} %volt.1, f32[128,128]{1,0:T(8,128)} %constant.12.clone.taps, f32[64,128]{1,0:T(8,128)} %constant.13.clone.twiddle, bf16[256,256]{1,0:T(8,128)(2,1)} %constant.14.clone.fine_upper, bf16[256,256]{1,0:T(8,128)(2,1)} %constant.15.clone.fine_lower, ...), custom_call_target="tpu_custom_call" | custom-call | flops 10000000000 | bytes 20000000 | tf_op jit(solution)/shard_map/pallas_call | solution.py:472
  127.2 1.0 copy.11
  128.2 0.3 reshape.6
  128.5 0.4 copy.12
  128.9 1.3 reshape.7

commit v5 on v4

--- a/solution.py
+++ b/solution.py
@@ -27,8 +27,7 @@
 SLOTS = SECTIONS * GROUPS
 STRIDE = 17
 LENGTH = BLOCKS_HERE * CHANNELS
-EARLY = 2 * CHANNELS
-LATE = CHANNELS
+HALO = TAPS - 1
 
 
 def tables():
@@ -186,9 +185,42 @@
     return total + jnp.dot(low, share, preferred_element_type=jnp.float32)
 
 
-def solve_packs(tile, first, count, weight, power, share, x, y, coeff, squares, diag):
-    own = pl.ds(pl.multiple_of(first * FEED_SETS, FEED_SETS), count * FEED_SETS)
-
+def own_rows(pack, count=1):
+    return pl.ds(pl.multiple_of(pack * FEED_SETS, FEED_SETS), count * FEED_SETS)
+
+
+def forward_pass(tile, count, x, coeff):
+    for pack in range(count):
+
+        def forward(index, inner):
+            pr = [jnp.zeros((GROUP, 128), jnp.float32) for _ in range(8)]
+            pi = [jnp.zeros((GROUP, 128), jnp.float32) for _ in range(8)]
+            for feed_set in range(FEED_SETS):
+                at = pack * FEED_SETS + feed_set
+                xr = x[0, at : at + 1, :]
+                xi = x[1, at : at + 1, :]
+                for two in range(4):
+                    re, im = tile(pack, index * 4 + two, feed_set)
+                    pr[two] = pr[two] + re * xr
+                    pr[4 + two] = pr[4 + two] + im * xi
+                    pi[two] = pi[two] + re * xi
+                    pi[4 + two] = pi[4 + two] - im * xr
+            at = pl.multiple_of((pack * SLOTS + index * 4) * GROUP, 4 * GROUP)
+            for two in range(4):
+                coeff[0, pl.ds(at + two * GROUP, GROUP), :] = pr[two] + pr[4 + two]
+                coeff[1, pl.ds(at + two * GROUP, GROUP), :] = pi[two] + pi[4 + two]
+            return inner
+
+        lax.fori_loop(0, SLOTS // 4, forward, 0)
+
+
+def start_x(first, count, weight, x):
+    span = slice(0, count * FEED_SETS)
+    x[0, span, :] = weight[own_rows(first, count), :]
+    x[1, span, :] = jnp.zeros((count * FEED_SETS, 128), jnp.float32)
+
+
+def start_packs(tile, first, count, weight, x, coeff, diag):
     def diagonal(feed_set, carry):
         for pack in range(count):
             total = [jnp.zeros((GROUP, 128), jnp.float32) for _ in range(4)]
@@ -203,10 +235,13 @@
         return carry
 
     lax.fori_loop(0, FEED_SETS, diagonal, 0)
+    start_x(first, count, weight, x)
+    forward_pass(tile, count, x, coeff)
+
+
+def solve_packs(tile, first, count, weight, power, share, x, y, coeff, squares, diag):
     span = slice(0, count * FEED_SETS)
-    diag[span, :] = float(SLOTS * GROUP) * power[own, :] - diag[span, :]
-    x[0, span, :] = weight[own, :]
-    x[1, span, :] = jnp.zeros((count * FEED_SETS, 128), jnp.float32)
+    diag[span, :] = float(SLOTS * GROUP) * power[own_rows(first, count), :] - diag[span, :]
     squares[...] = jnp.zeros_like(squares)
 
     def lengths():
@@ -214,28 +249,6 @@
         return [jnp.sqrt(total[8 * pack : 8 * pack + 1] + EPSILON) for pack in range(count)]
 
     def iterate(iteration, carry):
-        for pack in range(count):
-
-            def forward(index, inner):
-                pr = [jnp.zeros((GROUP, 128), jnp.float32) for _ in range(4)]
-                pi = [jnp.zeros((GROUP, 128), jnp.float32) for _ in range(4)]
-                for feed_set in range(FEED_SETS):
-                    at = pack * FEED_SETS + feed_set
-                    xr = x[0, at : at + 1, :]
-                    xi = x[1, at : at + 1, :]
-                    for two in range(2):
-                        re, im = tile(pack, index * 2 + two, feed_set)
-                        pr[two] = pr[two] + re * xr
-                        pr[2 + two] = pr[2 + two] + im * xi
-                        pi[two] = pi[two] + re * xi
-                        pi[2 + two] = pi[2 + two] - im * xr
-                at = pl.multiple_of((pack * SLOTS + index * 2) * GROUP, 2 * GROUP)
-                for two in range(2):
-                    coeff[0, pl.ds(at + two * GROUP, GROUP), :] = pr[two] + pr[2 + two]
-                    coeff[1, pl.ds(at + two * GROUP, GROUP), :] = pi[two] + pi[2 + two]
-                return inner
-
-            lax.fori_loop(0, SLOTS // 2, forward, 0)
         inverse = [jnp.where(iteration == 0, 1.0, 1.0 / length) for length in lengths()]
         for pack in range(count):
             rows = slice(pack * SLOTS * GROUP, (pack + 1) * SLOTS * GROUP)
@@ -265,8 +278,7 @@
             lax.fori_loop(0, FEED_SETS // 4, backward, 0)
         for pack in range(count):
             here = slice(pack * FEED_SETS, (pack + 1) * FEED_SETS)
-            at = pl.ds(pl.multiple_of((first + pack) * FEED_SETS, FEED_SETS), FEED_SETS)
-            w = weight[at, :]
+            w = weight[own_rows(first + pack), :]
             scaled = w * (diag[here, :] * (w * inverse[pack]))
             total = jnp.zeros((8, 128), jnp.float32)
             for part in range(2):
@@ -276,6 +288,11 @@
                     total = total + value[row : row + 8] * value[row : row + 8]
             total = jnp.sum(total, axis=0, keepdims=True)
             squares[8 * pack : 8 * pack + 8, :] = jnp.broadcast_to(total, (8, 128))
+
+        @pl.when(iteration < ITERS - 1)
+        def _():
+            forward_pass(tile, count, x, coeff)
+
         return carry
 
     lax.fori_loop(0, ITERS, iterate, 0)
@@ -287,7 +304,7 @@
 
 def kernel(
     volt, taps, twiddle, fine_upper, fine_lower, usable, auto_power, share, repeat, out,
-    weight, power, lined, ext, halfway, upper, lower, stage, sent_pair, sent_one, held_pair, held_one,
+    weight, power, lined, lined_back, wide, ext, halfway, upper, lower, stage, sent_pair, sent_one, held_pair, held_one,
     x, y, coeff, squares, diag, loads, send_sems, recv_sems, edge_sems,
 ):
     def arrange(source, target, split):
@@ -320,11 +337,39 @@
 
         lax.fori_loop(0, PACKS, body, 0)
 
+    def arrange_back(pack, rows):
+        feeds = FEED_SETS * FEEDS_HERE
+        lane = lax.broadcasted_iota(jnp.int32, (FEED_SETS, feeds), 1)
+        first = lax.broadcasted_iota(jnp.int32, (FEED_SETS, feeds), 0) * FEEDS_HERE
+        mine = (lane >= first) & (lane < first + FEEDS_HERE)
+        place = lax.broadcasted_iota(jnp.int32, (FEED_SETS, 128), 1)
+        dims = (((1,), (1,)), ((), ()))
+        for part in range(2):
+            value = x[part, rows, :]
+            for q in range(8):
+                own = (place >= q * FEEDS_HERE) & (place < (q + 1) * FEEDS_HERE)
+                lined_back[q * FEED_SETS : (q + 1) * FEED_SETS, :] = jnp.where(own, value, 0.0)
+            rest = lined_back[...]
+            total = jnp.zeros((8 * FEED_SETS, feeds), jnp.float32)
+            for _ in range(3):
+                piece = rest.astype(jnp.bfloat16)
+                rest = rest - piece.astype(jnp.float32)
+                total = total + lax.dot_general(
+                    piece, repeat[...], dims, preferred_element_type=jnp.float32
+                )
+            for q in range(8):
+                line = jnp.where(mine, total[q * FEED_SETS : (q + 1) * FEED_SETS], 0.0)
+                out[part, pl.ds(pack * 8 + q, 1), :] = jnp.sum(line, axis=0, keepdims=True)
+
     section = lax.axis_index("section")
     chan = lax.axis_index("chan")
+    core = lax.rem(chan, 2)
+    before = 2 - core
     me = section * FEED_SETS + chan
     sems = (send_sems, recv_sems)
-    load = pltpu.make_async_copy(volt, ext.at[:, :, pl.ds(EARLY, LENGTH)], loads)
+    load = pltpu.make_async_copy(
+        volt, ext.at[:, :, pl.ds(pl.multiple_of(before * CHANNELS, CHANNELS), LENGTH)], loads
+    )
     load.start()
     barrier = pltpu.get_barrier_semaphore()
 
@@ -334,24 +379,34 @@
         )
 
     visit(section, chan, greet)
-    early = copy_at(
-        volt.at[:, :, pl.ds(LENGTH - EARLY, EARLY)],
-        ext.at[:, :, pl.ds(0, EARLY)],
-        (edge_sems, edge_sems.at[pl.ds(2, 2)]),
-        0,
-        (lax.rem(section + 1, SECTIONS), chan),
-    )
-    late = copy_at(
-        volt.at[:, :, pl.ds(0, LATE)],
-        ext.at[:, :, pl.ds(EARLY + LENGTH, LATE)],
-        (edge_sems, edge_sems.at[pl.ds(2, 2)]),
-        1,
-        (lax.rem(section + SECTIONS - 1, SECTIONS), chan),
-    )
+    edges = []
+    for kind in range(2):
+        early, late = (2 - kind) * CHANNELS, (1 + kind) * CHANNELS
+        pair = (edge_sems, edge_sems.at[pl.ds(2, 2)])
+        edges.append((
+            copy_at(
+                volt.at[:, :, pl.ds(LENGTH - early, early)],
+                ext.at[:, :, pl.ds(0, early)],
+                pair,
+                0,
+                (lax.rem(section + 1, SECTIONS), chan),
+            ),
+            copy_at(
+                volt.at[:, :, pl.ds(0, late)],
+                ext.at[:, :, pl.ds(early + LENGTH, late)],
+                pair,
+                1,
+                (lax.rem(section + SECTIONS - 1, SECTIONS), chan),
+            ),
+        ))
     pl.semaphore_wait(barrier, OWNERS - 1)
-    early.start()
-    late.start()
-    arrange(usable, weight, False)
+    for kind in range(2):
+
+        @pl.when(core == kind)
+        def _():
+            edges[kind][0].start()
+            edges[kind][1].start()
+
     load.wait()
 
     def clear(first, count):
@@ -366,24 +421,27 @@
     def grouped(position, carry):
         group = lax.rem(position + 1, GROUPS)
 
-        @pl.when(position == 2)
+        for kind in range(2):
+
+            @pl.when((position == 2) & (core == kind))
+            def _():
+                edges[kind][1].wait()
+
+            @pl.when((position == 3) & (core == kind))
+            def _():
+                edges[kind][0].wait()
+
+        @pl.when((position == 3) & (section == 0))
         def _():
-            late.wait()
-
-        @pl.when(position == 3)
-        def _():
-            early.wait()
-
-            @pl.when(section == 0)
-            def _():
-                clear(0, 2)
+            clear(0, before)
 
         def step(at, inner):
             @pl.when((section == SECTIONS - 1) & (position == 2) & (at == GROUP - 1))
             def _():
-                clear(BLOCKS_HERE - 1, TAPS - 1)
-
-            first_transform(group * GROUP + at, ext, taps, halfway)
+                clear(BLOCKS_HERE - HALO + before, HALO)
+
+            block = lax.rem(group * GROUP + at + core * (BLOCKS_HERE - 1), BLOCKS_HERE)
+            first_transform(block, ext, taps, halfway)
             second_transform(twiddle, halfway, upper, lower)
             fine_transform(at, fine_upper, fine_lower, upper, lower, stage)
             return inner
@@ -408,15 +466,28 @@
 
     lax.fori_loop(0, GROUPS, grouped, 0)
 
-    def rest(pack, carry):
+    def send_third(there, column):
+        source = sent_one.at[0, there * FEED_SETS + column]
+        copy_at(source, held_one.at[0, me], sems, 1, (there, column)).start()
+
+    visit(section, chan, send_third)
+
+    def rest(group, carry):
         def send(there, column):
-            source = sent_one.at[pack, there * FEED_SETS + column]
-            copy_at(source, held_one.at[pack, me], sems, 1 + pack, (there, column)).start()
+            pltpu.make_async_remote_copy(
+                src_ref=sent_one.at[1, there * FEED_SETS + column, group],
+                dst_ref=held_one.at[1, me, group],
+                send_sem=send_sems.at[2],
+                recv_sem=recv_sems.at[2 + group],
+                device_id=(there, column),
+                device_id_type=pl.DeviceIdType.MESH,
+            ).start()
 
         visit(section, chan, send)
         return carry
 
-    lax.fori_loop(0, 2, rest, 0)
+    lax.fori_loop(0, GROUPS, rest, 0)
+    arrange(usable, weight, False)
     arrange(auto_power, power, True)
 
     for group in range(GROUPS):
@@ -432,25 +503,93 @@
         value = held_pair[source, lax.rem(slot, GROUPS), pack].astype(jnp.float32)
         return value[0:GROUP], value[GROUP:]
 
-    solve_packs(tile_pair, 0, 2, weight, power, share, x, y, coeff, squares, diag)
-    out[:, 0 : 2 * FEED_SETS, :] = x[...]
-
-    def single(index, carry):
+    first_row = lax.broadcasted_iota(jnp.int32, (16, 128), 0)
+    first_row = (first_row == 0) | (first_row == GROUP)
+
+    def mend(read, write):
+        def body(index, carry):
+            values = [read(at * FEED_SETS + 2 * index + 1).astype(jnp.float32) for at in range(4)]
+            for at in range(4):
+                value = jnp.where(first_row, values[at - 1], values[at])
+                write(at * FEED_SETS + 2 * index + 1, value.astype(jnp.bfloat16))
+            return carry
+
+        lax.fori_loop(0, FEED_SETS // 2, body, 0)
+
+    for pack in range(2):
+
+        def write_pair(source, value):
+            held_pair[source, 0, pack] = value
+
+        mend(lambda source: held_pair[source, 0, pack], write_pair)
+    scratch = (weight, power, share, x, y, coeff, squares, diag)
+    start_packs(tile_pair, 0, 2, weight, x, coeff, diag)
+    solve_packs(tile_pair, 0, 2, *scratch)
+    for pack in range(2):
+        arrange_back(pack, slice(pack * FEED_SETS, (pack + 1) * FEED_SETS))
+
+    def tile_third(pack, slot, feed_set):
+        source = lax.div(slot, GROUPS) * FEED_SETS + feed_set
+        value = held_one[0, source, lax.rem(slot, GROUPS)].astype(jnp.float32)
+        return value[0:GROUP], value[GROUP:]
+
+    def write_third(source, value):
+        held_one[0, source, 0] = value
+
+    pltpu.make_async_copy(
+        sent_one.at[0, others], held_one.at[0, others], recv_sems.at[1]
+    ).wait()
+    mend(lambda source: held_one[0, source, 0], write_third)
+    start_packs(tile_third, 2, 1, weight, x, coeff, diag)
+    solve_packs(tile_third, 2, 1, *scratch)
+    arrange_back(2, slice(0, FEED_SETS))
+
+    def tile_last(pack, slot, feed_set):
+        at = slot * FEED_SETS + feed_set
+        return wide[at, 0], wide[at, 1]
+
+    start_x(3, 1, weight, x)
+    diag[0:FEED_SETS, :] = jnp.zeros((FEED_SETS, 128), jnp.float32)
+    top_row = lax.broadcasted_iota(jnp.int32, (GROUP, 128), 0) == 0
+    for group in range(GROUPS):
         pltpu.make_async_copy(
-            sent_one.at[0, others], held_one.at[index, others], recv_sems.at[1 + index]
+            sent_one.at[1, others, group], held_one.at[1, others, group], recv_sems.at[2 + group]
         ).wait()
 
-        def tile_one(pack, slot, feed_set):
-            source = lax.div(slot, GROUPS) * FEED_SETS + feed_set
-            value = held_one[index, source, lax.rem(slot, GROUPS)].astype(jnp.float32)
-            return value[0:GROUP], value[GROUP:]
-
-        solve_packs(tile_one, 2 + index, 1, weight, power, share, x, y, coeff, squares, diag)
-        at = pl.multiple_of((2 + index) * FEED_SETS, FEED_SETS)
-        out[:, pl.ds(at, FEED_SETS), :] = x[:, 0:FEED_SETS, :]
-        return carry
-
-    lax.fori_loop(0, 2, single, 0)
+        def arrive(index, sums):
+            sums = list(sums)
+            for near in range(2):
+                feed_set = index * 2 + near
+                weight_row = x[0, pl.ds(feed_set, 1), :]
+                values = []
+                for at in range(SECTIONS):
+                    value = held_one[1, at * FEED_SETS + feed_set, group].astype(jnp.float32)
+                    values.append((value[0:GROUP], value[GROUP:]))
+                if group == 0 and near == 1:
+                    values = [
+                        tuple(jnp.where(top_row, values[at - 1][c], values[at][c]) for c in range(2))
+                        for at in range(SECTIONS)
+                    ]
+                total = jnp.zeros((GROUP, 128), jnp.float32)
+                for at, (re, im) in enumerate(values):
+                    place = (at * GROUPS + group) * FEED_SETS + feed_set
+                    wide[place, 0] = re
+                    wide[place, 1] = im
+                    total = total + (re * re + im * im)
+                    sums[2 * at] = sums[2 * at] + re * weight_row
+                    sums[2 * at + 1] = sums[2 * at + 1] - im * weight_row
+                row = pl.ds(feed_set, 1)
+                diag[row, :] = diag[row, :] + jnp.sum(total, axis=0, keepdims=True)
+            return tuple(sums)
+
+        zero = jnp.zeros((GROUP, 128), jnp.float32)
+        sums = lax.fori_loop(0, FEED_SETS // 2, arrive, (zero,) * (2 * SECTIONS))
+        for at in range(SECTIONS):
+            rows = slice((at * GROUPS + group) * GROUP, (at * GROUPS + group + 1) * GROUP)
+            coeff[0, rows, :] = sums[2 * at]
+            coeff[1, rows, :] = sums[2 * at + 1]
+    solve_packs(tile_last, 3, 1, *scratch)
+    arrange_back(3, slice(0, FEED_SETS))
     pltpu.make_async_copy(sent_pair.at[others], held_pair.at[others], send_sems.at[0]).wait()
     for pack in range(2):
         pltpu.make_async_copy(
@@ -469,16 +608,18 @@
     vmem = pl.BlockSpec(memory_space=pltpu.VMEM)
     pair = pltpu.VMEM((OWNERS, GROUPS, 2, 16, 128), jnp.bfloat16)
     one = pltpu.VMEM((2, OWNERS, GROUPS, 16, 128), jnp.bfloat16)
-    gains = pl.pallas_call(
+    return pl.pallas_call(
         kernel,
-        out_shape=jax.ShapeDtypeStruct((2, rows, 128), jnp.float32),
+        out_shape=jax.ShapeDtypeStruct((2, PACKS * 8, FEED_SETS * FEEDS_HERE), jnp.float32),
         in_specs=[pl.BlockSpec(memory_space=pl.ANY)] + [vmem] * 8,
         out_specs=vmem,
         scratch_shapes=[
             pltpu.VMEM((rows, 128), jnp.float32),
             pltpu.VMEM((rows, 128), jnp.float32),
             pltpu.VMEM((8 * FEED_SETS, FEED_SETS * FEEDS_HERE), jnp.float32),
-            pltpu.VMEM((2, FEEDS_HERE, EARLY + LENGTH + LATE), jnp.bfloat16),
+            pltpu.VMEM((8 * FEED_SETS, 128), jnp.float32),
+            pltpu.VMEM((SLOTS * FEED_SETS, 2, GROUP, 128), jnp.float32),
+            pltpu.VMEM((2, FEEDS_HERE, LENGTH + HALO * CHANNELS), jnp.bfloat16),
             pltpu.VMEM((4, 8, 2, FEEDS_HERE, FINE), jnp.float32),
             pltpu.VMEM((COARSE * FEEDS_HERE, 256), jnp.bfloat16),
             pltpu.VMEM((COARSE * FEEDS_HERE, 256), jnp.bfloat16),
@@ -494,7 +635,7 @@
             pltpu.VMEM((2 * FEED_SETS, 128), jnp.float32),
             pltpu.SemaphoreType.DMA,
             pltpu.SemaphoreType.DMA((3,)),
-            pltpu.SemaphoreType.DMA((3,)),
+            pltpu.SemaphoreType.DMA((2 + GROUPS,)),
             pltpu.SemaphoreType.DMA((4,)),
         ],
         compiler_params=pltpu.CompilerParams(
@@ -505,8 +646,6 @@
         voltages, taps, twiddle, upper, lower,
         usable, auto_power, share.astype(jnp.bfloat16), repeat,
     )
-    gains = gains.reshape(2, PACKS, FEED_SETS, 8, FEEDS_HERE).transpose(0, 1, 3, 2, 4)
-    return gains.reshape(2, PACKS * 8, FEED_SETS * FEEDS_HERE)
 
 
 def solution(mesh):

time: 130 us -> 130 us (level)
  the two profiles are of different devices: /device:TPU:1 before, /device:TPU:67 now
where the time goes in v5:
time: 130 us
  Pallas kernels  128 us (98%)
  local copies, waits for them, and re-layouts  1.57 us (1%)
    pallas_call x1, Pallas kernels, local(): pl.pallas_call(kernel, out_shape=jax.ShapeDtypeStruct((2, PACKS * 8, FEED...  128 us

profile of v5, /device:TPU:67, one launch (start us, length us, event | category | flops | bytes accessed | tf_op | source)
XLA Modules:
  0.0 130.0 jit_solution(9582223781469725685)
XLA Ops:
  0.0 128.4 %shard_map.91 = f32[2,32,512]{2,1,0:T(8,128)} custom-call(bf16[2,16,131072]{2,1,0:T(8,128)(2,1)} %volt.1, f32[128,128]{1,0:T(8,128)} %constant.12.clone.taps, f32[64,128]{1,0:T(8,128)} %constant.13.clone.twiddle, bf16[256,256]{1,0:T(8,128)(2,1)} %constant.14.clone.fine_upper, bf16[256,256]{1,0:T(8,128)(2,1)} %constant.15.clone.fine_lower, s32[32,512]{1,0:T(8,128)} %usable.1, ...), custom_call_target="tpu_custom_call" | custom-call | flops 10000000000 | bytes 20000000 | tf_op jit(solution)/shard_map/pallas_call | solution.py:611
  128.5 1.6 %copy.11 = f32[2,32,512]{2,1,0:T(8,128)} copy(f32[2,32,512]{2,1,0:T(8,128)} %shard_map.91) | data formatting | bytes 262144

commit v6 on v5

--- a/solution.py
+++ b/solution.py
@@ -218,25 +218,6 @@
     span = slice(0, count * FEED_SETS)
     x[0, span, :] = weight[own_rows(first, count), :]
     x[1, span, :] = jnp.zeros((count * FEED_SETS, 128), jnp.float32)
-
-
-def start_packs(tile, first, count, weight, x, coeff, diag):
-    def diagonal(feed_set, carry):
-        for pack in range(count):
-            total = [jnp.zeros((GROUP, 128), jnp.float32) for _ in range(4)]
-            for slot in range(SLOTS):
-                re, im = tile(pack, slot, feed_set)
-                at = slot % 2
-                total[at] = total[at] + re * re
-                total[2 + at] = total[2 + at] + im * im
-            total = (total[0] + total[1]) + (total[2] + total[3])
-            at = pl.ds(pack * FEED_SETS + feed_set, 1)
-            diag[at, :] = jnp.sum(total, axis=0, keepdims=True)
-        return carry
-
-    lax.fori_loop(0, FEED_SETS, diagonal, 0)
-    start_x(first, count, weight, x)
-    forward_pass(tile, count, x, coeff)
 
 
 def solve_packs(tile, first, count, weight, power, share, x, y, coeff, squares, diag):
@@ -366,7 +347,6 @@
     core = lax.rem(chan, 2)
     before = 2 - core
     me = section * FEED_SETS + chan
-    sems = (send_sems, recv_sems)
     load = pltpu.make_async_copy(
         volt, ext.at[:, :, pl.ds(pl.multiple_of(before * CHANNELS, CHANNELS), LENGTH)], loads
     )
@@ -458,8 +438,14 @@
         lax.fori_loop(0, OWNERS, emit, 0, unroll=8)
 
         def send(there, column):
-            source = sent_pair.at[there * FEED_SETS + column, group]
-            copy_at(source, held_pair.at[me, group], sems, 0, (there, column)).start()
+            pltpu.make_async_remote_copy(
+                src_ref=sent_pair.at[there * FEED_SETS + column, group],
+                dst_ref=held_pair.at[me, group],
+                send_sem=send_sems.at[0],
+                recv_sem=recv_sems.at[group],
+                device_id=(there, column),
+                device_id_type=pl.DeviceIdType.MESH,
+            ).start()
 
         visit(section, chan, send)
         return carry
@@ -467,8 +453,14 @@
     lax.fori_loop(0, GROUPS, grouped, 0)
 
     def send_third(there, column):
-        source = sent_one.at[0, there * FEED_SETS + column]
-        copy_at(source, held_one.at[0, me], sems, 1, (there, column)).start()
+        pltpu.make_async_remote_copy(
+            src_ref=sent_one.at[0, there * FEED_SETS + column],
+            dst_ref=held_one.at[0, me],
+            send_sem=send_sems.at[1],
+            recv_sem=recv_sems.at[2 * GROUPS],
+            device_id=(there, column),
+            device_id_type=pl.DeviceIdType.MESH,
+        ).start()
 
     visit(section, chan, send_third)
 
@@ -478,7 +470,7 @@
                 src_ref=sent_one.at[1, there * FEED_SETS + column, group],
                 dst_ref=held_one.at[1, me, group],
                 send_sem=send_sems.at[2],
-                recv_sem=recv_sems.at[2 + group],
+                recv_sem=recv_sems.at[GROUPS + group],
                 device_id=(there, column),
                 device_id_type=pl.DeviceIdType.MESH,
             ).start()
@@ -496,99 +488,83 @@
             held_one[pack, me, group] = sent_one[pack, me, group]
 
     others = pl.ds(0, OWNERS - 1)
-    pltpu.make_async_copy(sent_pair.at[others], held_pair.at[others], recv_sems.at[0]).wait()
-
-    def tile_pair(pack, slot, feed_set):
-        source = lax.div(slot, GROUPS) * FEED_SETS + feed_set
-        value = held_pair[source, lax.rem(slot, GROUPS), pack].astype(jnp.float32)
-        return value[0:GROUP], value[GROUP:]
-
-    first_row = lax.broadcasted_iota(jnp.int32, (16, 128), 0)
-    first_row = (first_row == 0) | (first_row == GROUP)
-
-    def mend(read, write):
-        def body(index, carry):
-            values = [read(at * FEED_SETS + 2 * index + 1).astype(jnp.float32) for at in range(4)]
-            for at in range(4):
-                value = jnp.where(first_row, values[at - 1], values[at])
-                write(at * FEED_SETS + 2 * index + 1, value.astype(jnp.bfloat16))
-            return carry
-
-        lax.fori_loop(0, FEED_SETS // 2, body, 0)
-
-    for pack in range(2):
-
-        def write_pair(source, value):
-            held_pair[source, 0, pack] = value
-
-        mend(lambda source: held_pair[source, 0, pack], write_pair)
     scratch = (weight, power, share, x, y, coeff, squares, diag)
-    start_packs(tile_pair, 0, 2, weight, x, coeff, diag)
-    solve_packs(tile_pair, 0, 2, *scratch)
+    top_row = lax.broadcasted_iota(jnp.int32, (GROUP, 128), 0) == 0
+
+    def tile(pack, slot, feed_set):
+        at = (pack * SLOTS + slot) * FEED_SETS + feed_set
+        return wide[at, 0], wide[at, 1]
+
+    def begin(first, count):
+        start_x(first, count, weight, x)
+        diag[0 : count * FEED_SETS, :] = jnp.zeros((count * FEED_SETS, 128), jnp.float32)
+
+    def take(read, group, count):
+        def arrive(index, sums):
+            sums = list(sums)
+            for pack in range(count):
+                for near in range(2):
+                    feed_set = index * 2 + near
+                    row = pl.ds(pack * FEED_SETS + feed_set, 1)
+                    weight_row = x[0, row, :]
+                    values = []
+                    for at in range(SECTIONS):
+                        value = read(at * FEED_SETS + feed_set, pack).astype(jnp.float32)
+                        values.append((value[0:GROUP], value[GROUP:]))
+                    if group == 0 and near == 1:
+                        values = [
+                            tuple(jnp.where(top_row, values[at - 1][c], values[at][c]) for c in range(2))
+                            for at in range(SECTIONS)
+                        ]
+                    total = jnp.zeros((GROUP, 128), jnp.float32)
+                    for at, (re, im) in enumerate(values):
+                        place = (pack * SLOTS + at * GROUPS + group) * FEED_SETS + feed_set
+                        wide[place, 0] = re
+                        wide[place, 1] = im
+                        total = total + (re * re + im * im)
+                        own = 2 * (pack * SECTIONS + at)
+                        sums[own] = sums[own] + re * weight_row
+                        sums[own + 1] = sums[own + 1] - im * weight_row
+                    diag[row, :] = diag[row, :] + jnp.sum(total, axis=0, keepdims=True)
+            return tuple(sums)
+
+        zero = jnp.zeros((GROUP, 128), jnp.float32)
+        sums = lax.fori_loop(0, FEED_SETS // 2, arrive, (zero,) * (2 * SECTIONS * count))
+        for pack in range(count):
+            for at in range(SECTIONS):
+                slot = pack * SLOTS + at * GROUPS + group
+                own = 2 * (pack * SECTIONS + at)
+                for part in range(2):
+                    coeff[part, slot * GROUP : (slot + 1) * GROUP, :] = sums[own + part]
+
+    begin(0, 2)
+    for group in (1, 2, 3, 0):
+        pltpu.make_async_copy(
+            sent_pair.at[others, group], held_pair.at[others, group], recv_sems.at[group]
+        ).wait()
+        take(lambda source, pack: held_pair[source, group, pack], group, 2)
+    solve_packs(tile, 0, 2, *scratch)
     for pack in range(2):
         arrange_back(pack, slice(pack * FEED_SETS, (pack + 1) * FEED_SETS))
 
-    def tile_third(pack, slot, feed_set):
-        source = lax.div(slot, GROUPS) * FEED_SETS + feed_set
-        value = held_one[0, source, lax.rem(slot, GROUPS)].astype(jnp.float32)
-        return value[0:GROUP], value[GROUP:]
-
-    def write_third(source, value):
-        held_one[0, source, 0] = value
-
+    begin(2, 1)
     pltpu.make_async_copy(
-        sent_one.at[0, others], held_one.at[0, others], recv_sems.at[1]
+        sent_one.at[0, others], held_one.at[0, others], recv_sems.at[2 * GROUPS]
     ).wait()
-    mend(lambda source: held_one[0, source, 0], write_third)
-    start_packs(tile_third, 2, 1, weight, x, coeff, diag)
-    solve_packs(tile_third, 2, 1, *scratch)
+    for group in range(GROUPS):
+        take(lambda source, pack: held_one[0, source, group], group, 1)
+    solve_packs(tile, 2, 1, *scratch)
     arrange_back(2, slice(0, FEED_SETS))
 
-    def tile_last(pack, slot, feed_set):
-        at = slot * FEED_SETS + feed_set
-        return wide[at, 0], wide[at, 1]
-
-    start_x(3, 1, weight, x)
-    diag[0:FEED_SETS, :] = jnp.zeros((FEED_SETS, 128), jnp.float32)
-    top_row = lax.broadcasted_iota(jnp.int32, (GROUP, 128), 0) == 0
+    begin(3, 1)
     for group in range(GROUPS):
         pltpu.make_async_copy(
-            sent_one.at[1, others, group], held_one.at[1, others, group], recv_sems.at[2 + group]
+            sent_one.at[1, others, group],
+            held_one.at[1, others, group],
+            recv_sems.at[GROUPS + group],
         ).wait()
-
-        def arrive(index, sums):
-            sums = list(sums)
-            for near in range(2):
-                feed_set = index * 2 + near
-                weight_row = x[0, pl.ds(feed_set, 1), :]
-                values = []
-                for at in range(SECTIONS):
-                    value = held_one[1, at * FEED_SETS + feed_set, group].astype(jnp.float32)
-                    values.append((value[0:GROUP], value[GROUP:]))
-                if group == 0 and near == 1:
-                    values = [
-                        tuple(jnp.where(top_row, values[at - 1][c], values[at][c]) for c in range(2))
-                        for at in range(SECTIONS)
-                    ]
-                total = jnp.zeros((GROUP, 128), jnp.float32)
-                for at, (re, im) in enumerate(values):
-                    place = (at * GROUPS + group) * FEED_SETS + feed_set
-                    wide[place, 0] = re
-                    wide[place, 1] = im
-                    total = total + (re * re + im * im)
-                    sums[2 * at] = sums[2 * at] + re * weight_row
-                    sums[2 * at + 1] = sums[2 * at + 1] - im * weight_row
-                row = pl.ds(feed_set, 1)
-                diag[row, :] = diag[row, :] + jnp.sum(total, axis=0, keepdims=True)
-            return tuple(sums)
-
-        zero = jnp.zeros((GROUP, 128), jnp.float32)
-        sums = lax.fori_loop(0, FEED_SETS // 2, arrive, (zero,) * (2 * SECTIONS))
-        for at in range(SECTIONS):
-            rows = slice((at * GROUPS + group) * GROUP, (at * GROUPS + group + 1) * GROUP)
-            coeff[0, rows, :] = sums[2 * at]
-            coeff[1, rows, :] = sums[2 * at + 1]
-    solve_packs(tile_last, 3, 1, *scratch)
+        take(lambda source, pack: held_one[1, source, group], group, 1)
+    solve_packs(tile, 3, 1, *scratch)
     arrange_back(3, slice(0, FEED_SETS))
     pltpu.make_async_copy(sent_pair.at[others], held_pair.at[others], send_sems.at[0]).wait()
     for pack in range(2):
@@ -618,7 +594,7 @@
             pltpu.VMEM((rows, 128), jnp.float32),
             pltpu.VMEM((8 * FEED_SETS, FEED_SETS * FEEDS_HERE), jnp.float32),
             pltpu.VMEM((8 * FEED_SETS, 128), jnp.float32),
-            pltpu.VMEM((SLOTS * FEED_SETS, 2, GROUP, 128), jnp.float32),
+            pltpu.VMEM((2 * SLOTS * FEED_SETS, 2, GROUP, 128), jnp.float32),
             pltpu.VMEM((2, FEEDS_HERE, LENGTH + HALO * CHANNELS), jnp.bfloat16),
             pltpu.VMEM((4, 8, 2, FEEDS_HERE, FINE), jnp.float32),
             pltpu.VMEM((COARSE * FEEDS_HERE, 256), jnp.bfloat16),
@@ -635,7 +611,7 @@
             pltpu.VMEM((2 * FEED_SETS, 128), jnp.float32),
             pltpu.SemaphoreType.DMA,
             pltpu.SemaphoreType.DMA((3,)),
-            pltpu.SemaphoreType.DMA((2 + GROUPS,)),
+            pltpu.SemaphoreType.DMA((1 + 2 * GROUPS,)),
             pltpu.SemaphoreType.DMA((4,)),
         ],
         compiler_params=pltpu.CompilerParams(

time: 130 us -> 129 us (level)
    pallas_call x1, Pallas kernels: 128 us -> 127 us  [local(): pl.pallas_call(kernel, out_shape=jax.ShapeDtypeStruct((2, PACKS * 8, FEED...]
where the time goes in v6:
time: 129 us
  Pallas kernels  127 us (98%)
  local copies, waits for them, and re-layouts  1.57 us (1%)
    pallas_call x1, Pallas kernels, local(): pl.pallas_call(kernel, out_shape=jax.ShapeDtypeStruct((2, PACKS * 8, FEED...  127 us

profile of v6, /device:TPU:67, one launch (start us, length us, event | category | flops | bytes accessed | tf_op | source)
XLA Modules:
  0.0 128.5 jit_solution(5817838087888850668)
XLA Ops:
  0.0 126.9 %shard_map.91 = f32[2,32,512]{2,1,0:T(8,128)} custom-call(bf16[2,16,131072]{2,1,0:T(8,128)(2,1)} %volt.1, f32[128,128]{1,0:T(8,128)} %constant.12.clone.taps, f32[64,128]{1,0:T(8,128)} %constant.13.clone.twiddle, bf16[256,256]{1,0:T(8,128)(2,1)} %constant.14.clone.fine_upper, bf16[256,256]{1,0:T(8,128)(2,1)} %constant.15.clone.fine_lower, s32[32,512]{1,0:T(8,128)} %usable.1, ...), custom_call_target="tpu_custom_call" | custom-call | flops 10000000000 | bytes 20000000 | tf_op jit(solution)/shard_map/pallas_call | solution.py:587
  127.0 1.6 %copy.11 = f32[2,32,512]{2,1,0:T(8,128)} copy(f32[2,32,512]{2,1,0:T(8,128)} %shard_map.91) | data formatting | bytes 262144

commit v7 on v6

--- a/solution.py
+++ b/solution.py
@@ -159,8 +159,8 @@
     several(*turns((0, 0, 0), same), 1)
 
     def body(step, carry):
-        near = [lax.rem(step, 2), lax.rem(lax.div(step, 2), 2), lax.rem(lax.div(step, 4), 2)]
-        core = lax.rem(same + lax.div(step, 8), 2)
+        near = [lax.rem(lax.div(step, 2), 2), lax.rem(lax.div(step, 4), 2), lax.rem(lax.div(step, 8), 2)]
+        core = lax.rem(same + step, 2)
         several(*turns(near, core), 0)
         return carry
 
@@ -332,7 +332,7 @@
                 lined_back[q * FEED_SETS : (q + 1) * FEED_SETS, :] = jnp.where(own, value, 0.0)
             rest = lined_back[...]
             total = jnp.zeros((8 * FEED_SETS, feeds), jnp.float32)
-            for _ in range(3):
+            for _ in range(2):
                 piece = rest.astype(jnp.bfloat16)
                 rest = rest - piece.astype(jnp.float32)
                 total = total + lax.dot_general(

time: 129 us -> 124 us (0.961)
  the two profiles are of different devices: /device:TPU:67 before, /device:TPU:1 now
where the time goes in v7:
time: 124 us
  Pallas kernels  122 us (98%)
  local copies, waits for them, and re-layouts  1.57 us (1%)
    pallas_call x1, Pallas kernels, local(): pl.pallas_call(kernel, out_shape=jax.ShapeDtypeStruct((2, PACKS * 8, FEED...  122 us

profile of v7, /device:TPU:1, one launch (start us, length us, event | category | flops | bytes accessed | tf_op | source)
XLA Modules:
  0.0 123.6 jit_solution(8026634923988852730)
XLA Ops:
  0.0 122.0 %shard_map.91 = f32[2,32,512]{2,1,0:T(8,128)} custom-call(bf16[2,16,131072]{2,1,0:T(8,128)(2,1)} %volt.1, f32[128,128]{1,0:T(8,128)} %constant.12.clone.taps, f32[64,128]{1,0:T(8,128)} %constant.13.clone.twiddle, bf16[256,256]{1,0:T(8,128)(2,1)} %constant.14.clone.fine_upper, bf16[256,256]{1,0:T(8,128)(2,1)} %constant.15.clone.fine_lower, s32[32,512]{1,0:T(8,128)} %usable.1, ...), custom_call_target="tpu_custom_call" | custom-call | flops 10000000000 | bytes 20000000 | tf_op jit(solution)/shard_map/pallas_call | solution.py:587
  122.0 1.6 %copy.11 = f32[2,32,512]{2,1,0:T(8,128)} copy(f32[2,32,512]{2,1,0:T(8,128)} %shard_map.91) | data formatting | bytes 262144

commit v8 on v7

--- a/solution.py
+++ b/solution.py
@@ -189,7 +189,7 @@
     return pl.ds(pl.multiple_of(pack * FEED_SETS, FEED_SETS), count * FEED_SETS)
 
 
-def forward_pass(tile, count, x, coeff):
+def forward_pass(tile, count, x, coeff, slots):
     for pack in range(count):
 
         def forward(index, inner):
@@ -211,7 +211,7 @@
                 coeff[1, pl.ds(at + two * GROUP, GROUP), :] = pi[two] + pi[4 + two]
             return inner
 
-        lax.fori_loop(0, SLOTS // 4, forward, 0)
+        lax.fori_loop(0, slots // 4, forward, 0)
 
 
 def start_x(first, count, weight, x):
@@ -220,9 +220,15 @@
     x[1, span, :] = jnp.zeros((count * FEED_SETS, 128), jnp.float32)
 
 
-def solve_packs(tile, first, count, weight, power, share, x, y, coeff, squares, diag):
+def solve_packs(
+    tile, first, count, weight, power, share, x, y, coeff, squares, diag, slots=SLOTS
+):
     span = slice(0, count * FEED_SETS)
-    diag[span, :] = float(SLOTS * GROUP) * power[own_rows(first, count), :] - diag[span, :]
+
+    def whole(value):
+        return value if slots == SLOTS else value + pltpu.roll(value, 64, 1)
+
+    diag[span, :] = float(SLOTS * GROUP) * power[own_rows(first, count), :] - whole(diag[span, :])
     squares[...] = jnp.zeros_like(squares)
 
     def lengths():
@@ -232,7 +238,7 @@
     def iterate(iteration, carry):
         inverse = [jnp.where(iteration == 0, 1.0, 1.0 / length) for length in lengths()]
         for pack in range(count):
-            rows = slice(pack * SLOTS * GROUP, (pack + 1) * SLOTS * GROUP)
+            rows = slice(pack * SLOTS * GROUP, (pack * SLOTS + slots) * GROUP)
             for part in range(2):
                 coeff[part, rows, :] = share_dot(coeff[part, rows, :], share[...]) * inverse[pack]
         for pack in range(count):
@@ -240,7 +246,7 @@
             def backward(index, inner):
                 yr = [jnp.zeros((GROUP, 128), jnp.float32) for _ in range(8)]
                 yi = [jnp.zeros((GROUP, 128), jnp.float32) for _ in range(8)]
-                for slot in range(SLOTS):
+                for slot in range(slots):
                     at = (pack * SLOTS + slot) * GROUP
                     pr = coeff[0, at : at + GROUP, :]
                     pi = coeff[1, at : at + GROUP, :]
@@ -263,7 +269,7 @@
             scaled = w * (diag[here, :] * (w * inverse[pack]))
             total = jnp.zeros((8, 128), jnp.float32)
             for part in range(2):
-                value = w * y[part, here, :] + scaled * x[part, here, :]
+                value = w * whole(y[part, here, :]) + scaled * x[part, here, :]
                 x[part, here, :] = value
                 for row in range(0, FEED_SETS, 8):
                     total = total + value[row : row + 8] * value[row : row + 8]
@@ -272,7 +278,7 @@
 
         @pl.when(iteration < ITERS - 1)
         def _():
-            forward_pass(tile, count, x, coeff)
+            forward_pass(tile, count, x, coeff, slots)
 
         return carry
 
@@ -285,7 +291,7 @@
 
 def kernel(
     volt, taps, twiddle, fine_upper, fine_lower, usable, auto_power, share, repeat, out,
-    weight, power, lined, lined_back, wide, ext, halfway, upper, lower, stage, sent_pair, sent_one, held_pair, held_one,
+    weight, power, lined, lined_back, wide, sent_half, held_half, kept, ext, halfway, upper, lower, stage, sent_pair, sent_one, held_pair, held_one,
     x, y, coeff, squares, diag, loads, send_sems, recv_sems, edge_sems,
 ):
     def arrange(source, target, split):
@@ -464,13 +470,32 @@
 
     visit(section, chan, send_third)
 
-    def rest(group, carry):
+    def low_lanes(shape):
+        return lax.broadcasted_iota(jnp.int32, shape, 1) < 64
+
+    def repack(owner, carry):
+        low = low_lanes((16, 128))
+        for pair in range(GROUPS // 2):
+            one, two = [
+                sent_one[1, owner, 2 * pair + at].astype(jnp.float32) for at in range(2)
+            ]
+            first = jnp.where(low, one, pltpu.roll(two, 64, 1))
+            second = jnp.where(low, pltpu.roll(one, 64, 1), two)
+            sent_half[0, owner, pair] = first.astype(jnp.bfloat16)
+            sent_half[1, owner, pair] = second.astype(jnp.bfloat16)
+        return carry
+
+    lax.fori_loop(0, OWNERS, repack, 0, unroll=4)
+
+    def rest(index, carry):
+        half, pair = lax.div(index, 2), lax.rem(index, 2)
+
         def send(there, column):
             pltpu.make_async_remote_copy(
-                src_ref=sent_one.at[1, there * FEED_SETS + column, group],
-                dst_ref=held_one.at[1, me, group],
+                src_ref=sent_half.at[half, there * FEED_SETS + column, pair],
+                dst_ref=held_half.at[half, me, pair],
                 send_sem=send_sems.at[2],
-                recv_sem=recv_sems.at[GROUPS + group],
+                recv_sem=recv_sems.at[GROUPS + index],
                 device_id=(there, column),
                 device_id_type=pl.DeviceIdType.MESH,
             ).start()
@@ -478,14 +503,21 @@
         visit(section, chan, send)
         return carry
 
-    lax.fori_loop(0, GROUPS, rest, 0)
+    lax.fori_loop(0, 4, rest, 0)
     arrange(usable, weight, False)
     arrange(auto_power, power, True)
+    for ref in (weight, power):
+        value = ref[own_rows(3), :]
+        other = pltpu.roll(value, 64, 1)
+        low = low_lanes((FEED_SETS, 128))
+        ref[own_rows(4), :] = jnp.where(low, value, other)
+        ref[own_rows(5), :] = jnp.where(low, other, value)
 
     for group in range(GROUPS):
         for pack in range(2):
             held_pair[me, group, pack] = sent_pair[me, group, pack]
-            held_one[pack, me, group] = sent_one[pack, me, group]
+            held_half[pack, me, group // 2] = sent_half[pack, me, group // 2]
+        held_one[0, me, group] = sent_one[0, me, group]
 
     others = pl.ds(0, OWNERS - 1)
     scratch = (weight, power, share, x, y, coeff, squares, diag)
@@ -499,7 +531,7 @@
         start_x(first, count, weight, x)
         diag[0 : count * FEED_SETS, :] = jnp.zeros((count * FEED_SETS, 128), jnp.float32)
 
-    def take(read, group, count):
+    def take(read, group, count, mend, per=GROUPS):
         def arrive(index, sums):
             sums = list(sums)
             for pack in range(count):
@@ -513,12 +545,12 @@
                         values.append((value[0:GROUP], value[GROUP:]))
                     if group == 0 and near == 1:
                         values = [
-                            tuple(jnp.where(top_row, values[at - 1][c], values[at][c]) for c in range(2))
+                            tuple(jnp.where(mend, values[at - 1][c], values[at][c]) for c in range(2))
                             for at in range(SECTIONS)
                         ]
                     total = jnp.zeros((GROUP, 128), jnp.float32)
                     for at, (re, im) in enumerate(values):
-                        place = (pack * SLOTS + at * GROUPS + group) * FEED_SETS + feed_set
+                        place = (pack * SLOTS + at * per + group) * FEED_SETS + feed_set
                         wide[place, 0] = re
                         wide[place, 1] = im
                         total = total + (re * re + im * im)
@@ -532,7 +564,7 @@
         sums = lax.fori_loop(0, FEED_SETS // 2, arrive, (zero,) * (2 * SECTIONS * count))
         for pack in range(count):
             for at in range(SECTIONS):
-                slot = pack * SLOTS + at * GROUPS + group
+                slot = pack * SLOTS + at * per + group
                 own = 2 * (pack * SECTIONS + at)
                 for part in range(2):
                     coeff[part, slot * GROUP : (slot + 1) * GROUP, :] = sums[own + part]
@@ -542,7 +574,7 @@
         pltpu.make_async_copy(
             sent_pair.at[others, group], held_pair.at[others, group], recv_sems.at[group]
         ).wait()
-        take(lambda source, pack: held_pair[source, group, pack], group, 2)
+        take(lambda source, pack: held_pair[source, group, pack], group, 2, top_row)
     solve_packs(tile, 0, 2, *scratch)
     for pack in range(2):
         arrange_back(pack, slice(pack * FEED_SETS, (pack + 1) * FEED_SETS))
@@ -552,19 +584,27 @@
         sent_one.at[0, others], held_one.at[0, others], recv_sems.at[2 * GROUPS]
     ).wait()
     for group in range(GROUPS):
-        take(lambda source, pack: held_one[0, source, group], group, 1)
+        take(lambda source, pack: held_one[0, source, group], group, 1, top_row)
     solve_packs(tile, 2, 1, *scratch)
     arrange_back(2, slice(0, FEED_SETS))
 
-    begin(3, 1)
-    for group in range(GROUPS):
-        pltpu.make_async_copy(
-            sent_one.at[1, others, group],
-            held_one.at[1, others, group],
-            recv_sems.at[GROUPS + group],
-        ).wait()
-        take(lambda source, pack: held_one[1, source, group], group, 1)
-    solve_packs(tile, 3, 1, *scratch)
+    for half in range(2):
+        begin(4 + half, 1)
+        for pair in range(2):
+            pltpu.make_async_copy(
+                sent_half.at[half, others, pair],
+                held_half.at[half, others, pair],
+                recv_sems.at[GROUPS + 2 * half + pair],
+            ).wait()
+            low = top_row & low_lanes((GROUP, 128))
+            take(lambda source, pack: held_half[half, source, pair], pair, 1, low, GROUPS // 2)
+        solve_packs(tile, 4 + half, 1, *scratch, slots=SLOTS // 2)
+        own = slice(0, FEED_SETS)
+        for part in range(2):
+            if half == 0:
+                kept[part] = x[part, own, :]
+            else:
+                x[part, own, :] = jnp.where(low_lanes((FEED_SETS, 128)), kept[part], x[part, own, :])
     arrange_back(3, slice(0, FEED_SETS))
     pltpu.make_async_copy(sent_pair.at[others], held_pair.at[others], send_sems.at[0]).wait()
     for pack in range(2):
@@ -583,6 +623,7 @@
     repeat = (lane == np.arange(128)[None, :] % FEEDS_HERE).astype(jnp.bfloat16)
     vmem = pl.BlockSpec(memory_space=pltpu.VMEM)
     pair = pltpu.VMEM((OWNERS, GROUPS, 2, 16, 128), jnp.bfloat16)
+    half = pltpu.VMEM((2, OWNERS, GROUPS // 2, 16, 128), jnp.bfloat16)
     one = pltpu.VMEM((2, OWNERS, GROUPS, 16, 128), jnp.bfloat16)
     return pl.pallas_call(
         kernel,
@@ -590,11 +631,14 @@
         in_specs=[pl.BlockSpec(memory_space=pl.ANY)] + [vmem] * 8,
         out_specs=vmem,
         scratch_shapes=[
-            pltpu.VMEM((rows, 128), jnp.float32),
-            pltpu.VMEM((rows, 128), jnp.float32),
+            pltpu.VMEM((rows + 2 * FEED_SETS, 128), jnp.float32),
+            pltpu.VMEM((rows + 2 * FEED_SETS, 128), jnp.float32),
             pltpu.VMEM((8 * FEED_SETS, FEED_SETS * FEEDS_HERE), jnp.float32),
             pltpu.VMEM((8 * FEED_SETS, 128), jnp.float32),
             pltpu.VMEM((2 * SLOTS * FEED_SETS, 2, GROUP, 128), jnp.float32),
+            half,
+            half,
+            pltpu.VMEM((2, FEED_SETS, 128), jnp.float32),
             pltpu.VMEM((2, FEEDS_HERE, LENGTH + HALO * CHANNELS), jnp.bfloat16),
             pltpu.VMEM((4, 8, 2, FEEDS_HERE, FINE), jnp.float32),
             pltpu.VMEM((COARSE * FEEDS_HERE, 256), jnp.bfloat16),

time: 124 us -> 124 us (level)
  the two profiles are of different devices: /device:TPU:1 before, /device:TPU:15 now
where the time goes in v8:
time: 124 us; the launch traced here: 123 us
  Pallas kernels  122 us (98%)
  local copies, waits for them, and re-layouts  1.57 us (1%)
    pallas_call x1, Pallas kernels, local(): pl.pallas_call(kernel, out_shape=jax.ShapeDtypeStruct((2, PACKS * 8, FEED...  122 us

profile of v8, /device:TPU:15, one launch (start us, length us, event | category | flops | bytes accessed | tf_op | source)
XLA Modules:
  0.0 123.5 jit_solution(849037725822134369)
XLA Ops:
  0.0 121.9 %shard_map.91 = f32[2,32,512]{2,1,0:T(8,128)} custom-call(bf16[2,16,131072]{2,1,0:T(8,128)(2,1)} %volt.1, f32[128,128]{1,0:T(8,128)} %constant.12.clone.taps, f32[64,128]{1,0:T(8,128)} %constant.13.clone.twiddle, bf16[256,256]{1,0:T(8,128)(2,1)} %constant.14.clone.fine_upper, bf16[256,256]{1,0:T(8,128)(2,1)} %constant.15.clone.fine_lower, s32[32,512]{1,0:T(8,128)} %usable.1, ...), custom_call_target="tpu_custom_call" | custom-call | flops 10000000000 | bytes 20000000 | tf_op jit(solution)/shard_map/pallas_call | solution.py:628
  121.9 1.6 %copy.11 = f32[2,32,512]{2,1,0:T(8,128)} copy(f32[2,32,512]{2,1,0:T(8,128)} %shard_map.91) | data formatting | bytes 262144

commit v9 on v8

--- a/solution.py
+++ b/solution.py
@@ -158,7 +158,8 @@
     same = lax.rem(chan, 2)
     several(*turns((0, 0, 0), same), 1)
 
-    def body(step, carry):
+    def body(index, carry):
+        step = index + same * (16 - 2 * index)
         near = [lax.rem(lax.div(step, 2), 2), lax.rem(lax.div(step, 4), 2), lax.rem(lax.div(step, 8), 2)]
         core = lax.rem(same + step, 2)
         several(*turns(near, core), 0)

time: 124 us -> 122 us (0.984)
  the two profiles are of different devices: /device:TPU:15 before, /device:TPU:1 now
where the time goes in v9:
time: 122 us
  Pallas kernels  120 us (98%)
  local copies, waits for them, and re-layouts  1.57 us (1%)
    pallas_call x1, Pallas kernels, local(): pl.pallas_call(kernel, out_shape=jax.ShapeDtypeStruct((2, PACKS * 8, FEED...  120 us

profile of v9, /device:TPU:1, one launch (start us, length us, event | category | flops | bytes accessed | tf_op | source)
XLA Modules:
  0.0 121.9 jit_solution(17878187817429827316)
XLA Ops:
  0.0 120.3 %shard_map.91 = f32[2,32,512]{2,1,0:T(8,128)} custom-call(bf16[2,16,131072]{2,1,0:T(8,128)(2,1)} %volt.1, f32[128,128]{1,0:T(8,128)} %constant.12.clone.taps, f32[64,128]{1,0:T(8,128)} %constant.13.clone.twiddle, bf16[256,256]{1,0:T(8,128)(2,1)} %constant.14.clone.fine_upper, bf16[256,256]{1,0:T(8,128)(2,1)} %constant.15.clone.fine_lower, s32[32,512]{1,0:T(8,128)} %usable.1, ...), custom_call_target="tpu_custom_call" | custom-call | flops 10000000000 | bytes 20000000 | tf_op jit(solution)/shard_map/pallas_call | solution.py:629
  120.4 1.6 %copy.11 = f32[2,32,512]{2,1,0:T(8,128)} copy(f32[2,32,512]{2,1,0:T(8,128)} %shard_map.91) | data formatting | bytes 262144

commit v10 on v9

--- a/solution.py
+++ b/solution.py
@@ -159,7 +159,8 @@
     several(*turns((0, 0, 0), same), 1)
 
     def body(index, carry):
-        step = index + same * (16 - 2 * index)
+        mixed = lax.rem(index * 5, 16)
+        step = mixed + same * (16 - 2 * mixed)
         near = [lax.rem(lax.div(step, 2), 2), lax.rem(lax.div(step, 4), 2), lax.rem(lax.div(step, 8), 2)]
         core = lax.rem(same + step, 2)
         several(*turns(near, core), 0)

time: 122 us -> 122 us (level)
  no operation moved by 1% of the time
where the time goes in v10:
time: 122 us
  Pallas kernels  120 us (98%)
  local copies, waits for them, and re-layouts  1.57 us (1%)
    pallas_call x1, Pallas kernels, local(): pl.pallas_call(kernel, out_shape=jax.ShapeDtypeStruct((2, PACKS * 8, FEED...  120 us

profile of v10, /device:TPU:1, one launch (start us, length us, event | category | flops | bytes accessed | tf_op | source)
XLA Modules:
  0.0 121.9 jit_solution(3534177051482333625)
XLA Ops:
  0.0 120.3 %shard_map.91 = f32[2,32,512]{2,1,0:T(8,128)} custom-call(bf16[2,16,131072]{2,1,0:T(8,128)(2,1)} %volt.1, f32[128,128]{1,0:T(8,128)} %constant.12.clone.taps, f32[64,128]{1,0:T(8,128)} %constant.13.clone.twiddle, bf16[256,256]{1,0:T(8,128)(2,1)} %constant.14.clone.fine_upper, bf16[256,256]{1,0:T(8,128)(2,1)} %constant.15.clone.fine_lower, s32[32,512]{1,0:T(8,128)} %usable.1, ...), custom_call_target="tpu_custom_call" | custom-call | flops 10000000000 | bytes 20000000 | tf_op jit(solution)/shard_map/pallas_call | solution.py:630
  120.3 1.6 %copy.11 = f32[2,32,512]{2,1,0:T(8,128)} copy(f32[2,32,512]{2,1,0:T(8,128)} %shard_map.91) | data formatting | bytes 262144
